TPU v7x, 32 devices: a 4x4x1 block of a 4x4x8 slice. The times are simulated.
32 devices in a mesh: dp: 1 (over z), dcp: 32 (over y, x, core).
Axes of the slice: x: 4, y: 4, z: 1, core: 2. Of those that a mesh axis runs over, the one named last changes fastest.
The devices are a block of a 4x4x8 slice.
Arguments:
- q: bfloat16 [64, 128, 576], P('dp', 'dcp')
- cache: bfloat16 [64, 64, 32, 8, 576], P('dp', None, 'dcp')
- lens: int32 [64], P('dp')
Outputs:
- output: bfloat16 [64, 128, 512], P('dp', 'dcp')
All inputs are finite; a program needn't handle non-finite values.
Results may differ from a plain program's by a relative error of at most 0.00773808.
Values are sent between devices in bfloat16 or wider.
A program may use at most 768 MiB of HBM per device.

v0:
```python
import jax
import jax.numpy as jnp
from jax import lax
from jax.sharding import PartitionSpec as P

ROPE = 64
QK_DIM = 192
SCALE = QK_DIM ** -0.5


def solution(mesh):
    n = mesh.shape['dcp']

    def local(q, cache, lens):
        b, hl, k = q.shape
        r = cache.shape[1]
        page = cache.shape[3]
        lorav = k - ROPE
        d = lax.axis_index('dcp')
        qa = lax.all_gather(q, 'dcp', axis=1, tiled=True)
        c = cache.reshape(b, r * page, k)
        pos = (jnp.arange(r)[:, None] * n + d) * page + jnp.arange(page)[None, :]
        valid = pos.reshape(r * page)[None, :] < lens[:, None]
        s = jnp.einsum('bhk,btk->bht', qa, c, preferred_element_type=jnp.float32) * SCALE
        s = jnp.where(valid[:, None, :], s, -jnp.inf)
        m = jnp.max(s, axis=2)
        m = jnp.where(jnp.isfinite(m), m, 0.0)
        p = jnp.exp(s - m[:, :, None])
        l = jnp.sum(p, axis=2)
        has = l > 0.0
        lsafe = jnp.where(has, l, 1.0)
        pv = jnp.einsum('bht,btk->bhk', p.astype(jnp.bfloat16), c[:, :, :lorav], preferred_element_type=jnp.float32)
        od = (pv / lsafe[:, :, None]).astype(jnp.bfloat16)
        lse = jnp.where(has, m + jnp.log(lsafe), -jnp.inf)
        od = lax.all_to_all(od.reshape(b, n, hl, lorav), 'dcp', 1, 1, tiled=True)
        lse = lax.all_to_all(lse.reshape(b, n, hl), 'dcp', 1, 1, tiled=True)
        top = jnp.max(lse, axis=1)
        w = jnp.exp(lse - top[:, None, :])
        o = jnp.sum(w[:, :, :, None] * od.astype(jnp.float32), axis=1) / jnp.sum(w, axis=1)[:, :, None]
        return o.astype(jnp.bfloat16)

    return jax.shard_map(local, mesh=mesh, in_specs=(P('dp', 'dcp', None), P('dp', None, 'dcp', None, None), P('dp')), out_specs=P('dp', 'dcp', None), check_vma=False)
```

profile of v0, /device:TPU:103, one launch (start us, length us, event | category | flops | bytes accessed | tf_op | source)
XLA Modules:
  0.0 279.7 jit_solution(9730942361555846279)
XLA Ops:
  6.6 1.7 copy.9
  8.3 0.1 all-gather.2.cloned.1.call-update
  8.3 0.1 iota_add_fusion
  8.4 0.1 add.40
  8.5 0.7 broadcast_compare_fusion
  9.3 55.4 %all-gather.2.cloned.1.call-done = bf16[64,128,576]{2,0,1:T(8,128)(2,1)} async-done(((bf16[64,4,576]{2,0,1:T(8,128)(2,1)}), bf16[64,128,576]{2,0,1:T(8,128)(2,1)}) %all-gather.2.cloned.1.call-update) | async-done | bytes 9437200 | tf_op jit(solution)/shard_map/all_gather | solution.py:20
  64.7 25.5 %fusion.2 = (f32[64,128]{1,0:T(8,128)S(1)}, f32[64,128,512]{2,1,0:T(8,128)}) fusion(pred[64,512]{1,0:T(8,128)(4,1)S(1)} %broadcast_compare_fusion, bf16[64,64,1,8,576]{4,3,2,1,0:T(8,128)(2,1)} %param.4, bf16[64,128,576]{2,0,1:T(8,128)(2,1)} %all-gather.2.cloned.1.call-done), kind=kOutput, calls=%fused_computation.6 | convolution fusion | flops 4844412928 | bytes 64028672 | tf_op jit(solution)/shard_map/bhk,btk->bht/dot_general | solution.py:24
  90.2 0.1 copy.13
  90.3 8.3 %fusion.4 = f32[64,128]{1,0:T(8,128)S(1)} fusion(f32[64,128,512]{2,1,0:T(8,128)} %get-tuple-element.8, f32[64,128]{1,0:T(8,128)S(1)} %is-finite_select_fusion.1, pred[64,512]{1,0:T(8,128)(4,1)S(1)} %broadcast_compare_fusion), kind=kLoop, calls=%fused_computation.8 | loop fusion | flops 16769024 | bytes 16875520 | tf_op jit(solution)/shard_map/reduce_sum | solution.py:29
  98.7 0.1 copy.12
  98.8 0.7 reshape.68
  99.5 4.5 %all-to-all-start = ((f32[32,1,256]{2,1,0:T(1,128)}), f32[32,1,256]{2,1,0:T(1,128)S(1)}, u32[]{:S(2)}, u32[]{:S(2)}) async-start(f32[32,1,256]{2,1,0:T(1,128)} %reshape.68), calls=%async_computation | async-start | bytes 65536 | tf_op jit(solution)/shard_map/all_to_all | solution.py:36
  104.1 21.2 %divide_convert_fusion = bf16[64,128,512]{2,1,0:T(8,128)(2,1)} fusion(bf16[64,512,576]{2,1,0:T(8,128)(2,1)} %bitcast.12, f32[64,128,512]{2,1,0:T(8,128)} %get-tuple-element.8, f32[64,128]{1,0:T(8,128)S(1)} %compare_select_fusion, f32[64,128]{1,0:T(8,128)S(1)} %is-finite_select_fusion.1, pred[64,512]{1,0:T(8,128)(4,1)S(1)} %broadcast_compare_fusion), kind=kOutput, calls=%fused_computation.3 | convolution fusion | flops 4320133120 | bytes 58818560 | tf_op jit(solution)/shard_map/bht,btk->bhk/dot_general | solution.py:32
  125.3 12.6 %reshape.67 = bf16[64,32,4,512]{3,2,1,0:T(4,128)(2,1)} reshape(bf16[64,128,512]{2,1,0:T(8,128)(2,1)} %divide_convert_fusion) | data formatting | bytes 16777216 | tf_op jit(solution)/shard_map/reshape | solution.py:35
  137.8 8.1 %copy.15 = bf16[64,32,4,512]{3,2,0,1:T(4,128)(2,1)} copy(bf16[64,32,4,512]{3,2,1,0:T(4,128)(2,1)} %reshape.67) | data formatting | bytes 16777216 | tf_op jit(solution)/shard_map/reshape | solution.py:35
  146.0 6.3 %all-to-all-start.1 = ((bf16[64,32,4,512]{3,2,0,1:T(4,128)(2,1)}), bf16[64,32,4,512]{3,2,0,1:T(4,128)(2,1)}, u32[]{:S(2)}, u32[]{:S(2)}) async-start(bf16[64,32,4,512]{3,2,0,1:T(4,128)(2,1)} %copy.15), calls=%async_computation.1 | async-start | bytes 16777216 | tf_op jit(solution)/shard_map/all_to_all | solution.py:35
  152.3 0.5 broadcast.53
  152.8 0.7 reduce
  153.6 0.1 reshape.69
  153.7 0.4 copy.14
  154.1 0.1 copy.16
  154.2 111.2 %all-to-all-done.1 = bf16[64,32,4,512]{3,2,0,1:T(4,128)(2,1)} async-done(((bf16[64,32,4,512]{3,2,0,1:T(4,128)(2,1)}), bf16[64,32,4,512]{3,2,0,1:T(4,128)(2,1)}, u32[]{:S(2)}, u32[]{:S(2)}) %all-to-all-start.1) | async-done | bytes 8388640 | tf_op jit(solution)/shard_map/all_to_all | solution.py:35
  265.5 6.5 %multiply_reduce_fusion = f32[64,4,512]{2,1,0:T(4,128)S(1)} fusion(bf16[64,32,4,512]{3,2,0,1:T(4,128)(2,1)} %all-to-all-done.1, f32[64,32,4]{2,0,1:T(8,128)S(1)} %copy.14), kind=kLoop, calls=%fused_computation.2 | loop fusion | flops 12451840 | bytes 8945664 | tf_op jit(solution)/shard_map/reduce_sum | solution.py:39
  271.9 0.9 divide_convert_fusion.1
  (8 shorter events, 0.2 us)
Async XLA Ops:
  6.5 58.1 %all-gather.2.cloned.1.call-start = ((), (), s32[]{:S(2)}) async-start(), calls=%async_computation.2 | async-start | bytes 10813440 | tf_op jit(solution)/shard_map/all_gather | solution.py:20
  99.5 46.4 %all-to-all-start = ((f32[32,1,256]{2,1,0:T(1,128)}), f32[32,1,256]{2,1,0:T(1,128)S(1)}, u32[]{:S(2)}, u32[]{:S(2)}) async-start(f32[32,1,256]{2,1,0:T(1,128)} %reshape.68), calls=%async_computation | async-start | bytes 65536 | tf_op jit(solution)/shard_map/all_to_all | solution.py:36
  146.0 119.5 %all-to-all-start.1 = ((bf16[64,32,4,512]{3,2,0,1:T(4,128)(2,1)}), bf16[64,32,4,512]{3,2,0,1:T(4,128)(2,1)}, u32[]{:S(2)}, u32[]{:S(2)}) async-start(bf16[64,32,4,512]{3,2,0,1:T(4,128)(2,1)} %copy.15), calls=%async_computation.1 | async-start | bytes 16777216 | tf_op jit(solution)/shard_map/all_to_all | solution.py:35
Sparse Core Ops, SparseCore 0:
  9.4 55.2 all-gather.1
where the time goes:
time: 280 us
  waiting for transfers between devices  167 us (60%)
  matrix products  46.7 us (17%)
  local copies, waits for them, and re-layouts  24.5 us (9%)
  other arithmetic  17.4 us (6%)
  between operations  13.5 us (5%)
  starting transfers between devices  10.8 us (4%)
    all_to_all x1, waiting for transfers between devices, local(): od = lax.all_to_all(od.reshape(b, n, hl, lorav), 'dcp', 1, 1, tiled=True)  111 us
    all_gather x1, waiting for transfers between devices, local(): qa = lax.all_gather(q, 'dcp', axis=1, tiled=True)  55.4 us
    dot_general x1, matrix products, local(): jnp.einsum('bhk,btk->bht', qa, c, preferred_element_type=jnp.float32)  25.5 us
    dot_general x1, matrix products, local(): jnp.einsum('bht,btk->bhk', p.astype(jnp.bfloat16), c[:, :, :lorav], prefe...  21.2 us
    reshape x2, local copies, waits for them, and re-layouts, local(): od = lax.all_to_all(od.reshape(b, n, hl, lorav), 'dcp', 1, 1, tiled=True)  20.7 us
    reduce_sum x1, other arithmetic, local(): l = jnp.sum(p, axis=2)  8.35 us
    reduce_sum x1, other arithmetic, local(): jnp.sum(w[:, :, :, None] * od.astype(jnp.float32), axis=1)  6.47 us
    all_to_all x1, starting transfers between devices, local(): od = lax.all_to_all(od.reshape(b, n, hl, lorav), 'dcp', 1, 1, tiled=True)  6.32 us
  transfers between devices with their start and end apart: 3, of which 2 were waited for; matrix products, arithmetic and copies ran while one was open for 16% of the time, Pallas kernels for 0%

commit v1 on v0

v1 whole, which is shorter than its diff:
```python
import functools
import math

import jax
import jax.numpy as jnp
from jax import lax
from jax.experimental import pallas as pl
from jax.experimental.pallas import tpu as pltpu
from jax.sharding import PartitionSpec as P

ROPE = 64
QK_DIM = 192
SCALE = QK_DIM ** -0.5
NEG = float('-inf')
LANES = 128
NBUF = 4


def kernel(n, side, nc, nb, page, q_ref, cache_ref, lens_ref, out_ref,
           g1, qall, cbuf, own, osend, orecv, p1s, p1r, l1s, l1r, p2s, p2r, l2s, l2r, wrow,
           csem, a1s, a1r, a2s, a2r, a3s, a3r, ods, odr, s1, r1, sl1, rl1, s2, r2, sl2, rl2):
    hl = q_ref.shape[1]
    k = q_ref.shape[2]
    t = cbuf.shape[1]
    lorav = k - ROPE
    tile = side * hl
    half = side * tile
    total = nc * nb

    me = lax.axis_index('dcp')
    core = me % 2
    x = (me // 2) % side
    y = me // (2 * side)
    dists = tuple(range(1, side))

    def at(yy, xx, cc):
        return {'dcp': (yy * side + xx) * 2 + cc}

    sib = at(y, x, 1 - core)

    def axes(c):
        ax = (x, lambda d: at(y, (x + d) % side, core))
        ay = (y, lambda d: at((y + d) % side, x, core))
        return (ax, ay) if c % 2 == 0 else (ay, ax)

    def rcopy(src, dst, ss, rs, dev):
        return pltpu.make_async_remote_copy(src_ref=src, dst_ref=dst, send_sem=ss, recv_sem=rs, device_id=dev,
                                            device_id_type=pl.DeviceIdType.MESH)

    def ag1(c, d):
        (m1, peer), _ = axes(c)
        return rcopy(q_ref.at[pl.ds(c * nb, nb)], g1.at[c, m1], a1s.at[c, d - 1], a1r.at[c, d - 1], peer(d))

    def ag2(c, d):
        _, (m2, peer) = axes(c)
        return rcopy(qall.at[c, m2], qall.at[c, m2], a2s.at[c, d - 1], a2r.at[c, d - 1], peer(d))

    def ag3(c, d):
        _, (m2, _) = axes(c)
        a = (m2 + side - d) % side
        return rcopy(qall.at[c, a], qall.at[c, side + a], a3s.at[c, d], a3r.at[c, d], sib)

    def od(c):
        return rcopy(osend.at[c % 2], orecv.at[c], ods.at[c], odr.at[c], sib)

    def rs1(c, d):
        _, (m2, peer) = axes(c)
        a = (m2 + d) % side
        return (rcopy(p1s.at[c, a], p1r.at[c, m2], s1.at[c, d - 1], r1.at[c, d - 1], peer(d)),
                rcopy(l1s.at[c], l1r.at[c, m2], sl1.at[c, d - 1], rl1.at[c, d - 1], peer(d)))

    def rs2(c, d):
        (m1, peer), _ = axes(c)
        a = (m1 + d) % side
        return (rcopy(p2s.at[c, a], p2r.at[c, m1], s2.at[c, d - 1], r2.at[c, d - 1], peer(d)),
                rcopy(l2s.at[c], l2r.at[c, m1], sl2.at[c, d - 1], rl2.at[c, d - 1], peer(d)))

    def cload(b):
        return pltpu.make_async_copy(cache_ref.at[b], cbuf.at[b % NBUF], csem.at[b % NBUF])

    for b in range(min(NBUF, total)):
        cload(b).start()

    barrier = pltpu.get_barrier_semaphore()
    peers = [sib] + [at(y, (x + d) % side, core) for d in dists] + [at((y + d) % side, x, core) for d in dists]
    for dev in peers:
        pl.semaphore_signal(barrier, inc=1, device_id=dev, device_id_type=pl.DeviceIdType.MESH)
    pl.semaphore_wait(barrier, len(peers))

    order = sorted(dists, key=lambda d: min(d, side - d))
    for c in range(nc):
        for d in order:
            ag1(c, d).start()

    def gather_first(c):
        (m1, _), (m2, _) = axes(c)
        g1[c, m1] = q_ref[pl.ds(c * nb, nb)]
        for d in order:
            ag1(c, d).wait_recv()

        def body(i, _):
            parts = [g1[c, a, i].astype(jnp.float32) for a in range(side)]
            qall[c, m2, i] = jnp.concatenate(parts, axis=0).astype(qall.dtype)
            return 0

        lax.fori_loop(0, nb, body, 0)
        for d in order:
            ag2(c, d).start()
        ag3(c, 0).start()

    def gather_second(c):
        for d in order:
            ag2(c, d).wait_recv()
            ag3(c, d).start()

    def gather_third(c):
        for d in range(side):
            ag3(c, d).wait_recv()

    tpos = lax.broadcasted_iota(jnp.int32, (1, t), 1)
    pos = (tpos // page) * (page * n) + me * page + tpos % page

    def compute(c):
        if c >= 2:
            od(c - 2).wait_send()

        def one(i, _):
            b = c * nb + i
            slot = b % NBUF
            cload(b).wait()
            qb = qall[c, :, i].reshape(2 * half, k)
            cb = cbuf[slot]
            s = lax.dot_general(qb, cb, (((1,), (1,)), ((), ())), preferred_element_type=jnp.float32)
            s = jnp.where(pos < lens_ref[b], s, NEG)
            m = jnp.max(s, axis=1, keepdims=True)
            ms = jnp.where(m == NEG, 0.0, m)
            p = jnp.exp((s - ms) * SCALE)
            l = jnp.sum(p, axis=1, keepdims=True)
            acc = lax.dot_general(p.astype(jnp.bfloat16), cb[:, :lorav], (((1,), (0,)), ((), ())),
                                  preferred_element_type=jnp.float32)
            ls = jnp.where(l > 0.0, l, 1.0)
            o = acc * (1.0 / ls)
            lse = jnp.broadcast_to(jnp.where(l > 0.0, ms * SCALE + jnp.log(ls), NEG), (2 * half, LANES))
            own[c % 2, i, :, :lorav] = o[:half]
            own[c % 2, i, :, lorav:] = lse[:half]
            osend[c % 2, i, :, :lorav] = o[half:]
            osend[c % 2, i, :, lorav:] = lse[half:]

            @pl.when(b + NBUF < total)
            def _():
                cload(b + NBUF).start()

            return 0

        lax.fori_loop(0, nb, one, 0)
        od(c).start()

    diag = lax.broadcasted_iota(jnp.int32, (half, LANES), 0) == lax.broadcasted_iota(jnp.int32, (half, LANES), 1)

    def pair(c):
        od(c).wait_recv()

        def one(i, _):
            la = own[c % 2, i, :, lorav:]
            lb = orecv[c, i, :, lorav:]
            top = jnp.maximum(la, lb)
            ts = jnp.where(top == NEG, 0.0, top)
            wa = jnp.exp(la - ts)
            wb = jnp.exp(lb - ts)
            ws = wa + wb
            wss = jnp.where(ws > 0.0, ws, 1.0)
            inv = 1.0 / wss
            wa = wa * inv
            wb = wb * inv
            for j in range(lorav // LANES):
                cols = slice(j * LANES, (j + 1) * LANES)
                v = (wa * own[c % 2, i, :, cols] + wb * orecv[c, i, :, cols]).astype(jnp.bfloat16)
                p1s[c, :, i, :, cols] = v.reshape(side, tile, LANES)
            lse = jnp.where(ws > 0.0, ts + jnp.log(wss), NEG)
            l1s[c, pl.ds(i, 1)] = jnp.sum(jnp.where(diag, lse, 0.0), axis=0, keepdims=True)
            return 0

        lax.fori_loop(0, nb, one, 0)
        for d in order:
            for cp in rs1(c, d):
                cp.start()

    def weights(ls):
        top = functools.reduce(jnp.maximum, ls)
        ts = jnp.where(top == NEG, 0.0, top)
        w = [jnp.exp(v - ts) for v in ls]
        ws = functools.reduce(jnp.add, w)
        wss = jnp.where(ws > 0.0, ws, 1.0)
        inv = 1.0 / wss
        for j, v in enumerate(w):
            wrow[j] = v * inv
        return jnp.where(ws > 0.0, ts + jnp.log(wss), NEG)

    def combine(i, rows, first, srcs):
        sel = (lax.broadcasted_iota(jnp.int32, (rows, LANES), 0) + first
               == lax.broadcasted_iota(jnp.int32, (rows, LANES), 1))
        tot = None
        for j, src in enumerate(srcs):
            w = jnp.broadcast_to(wrow[j, pl.ds(i, 1)], (rows, LANES))
            w = jnp.sum(jnp.where(sel, w, 0.0), axis=1, keepdims=True)
            term = w * src[i].astype(jnp.float32)
            tot = term if tot is None else tot + term
        return tot

    def second(c):
        (m1, _), (m2, _) = axes(c)
        for d in order:
            for cp in rs1(c, d):
                cp.wait_recv()
        idx = [(m2 + d) % side for d in dists]
        l2s[c] = weights([l1s[c]] + [l1r[c, a] for a in idx])
        srcs = [p1s.at[c, m2]] + [p1r.at[c, a] for a in idx]

        def one(i, _):
            v = combine(i, tile, m2 * tile, srcs)
            for a in range(side):
                p2s[c, a, i] = v[a * hl:(a + 1) * hl]
            return 0

        lax.fori_loop(0, nb, one, 0)
        for d in order:
            for cp in rs2(c, d):
                cp.start()

    def final(c):
        (m1, _), (m2, _) = axes(c)
        for d in order:
            for cp in rs2(c, d):
                cp.wait_recv()
        idx = [(m1 + d) % side for d in dists]
        weights([l2s[c]] + [l2r[c, a] for a in idx])
        srcs = [p2s.at[c, m1]] + [p2r.at[c, a] for a in idx]

        def one(i, _):
            out_ref[c * nb + i] = combine(i, hl, m2 * tile + m1 * hl, srcs).astype(out_ref.dtype)
            return 0

        lax.fori_loop(0, nb, one, 0)

    for c in range(nc):
        gather_first(c)
    gather_second(0)
    for c in range(nc + 3):
        if c + 1 < nc:
            gather_second(c + 1)
        if c < nc:
            gather_third(c)
            compute(c)
        if 0 <= c - 1 < nc:
            pair(c - 1)
        if 0 <= c - 2 < nc:
            second(c - 2)
        if 0 <= c - 3 < nc:
            final(c - 3)
    for c in range(nc):
        for d in dists:
            ag1(c, d).wait_send()
            ag2(c, d).wait_send()
            for cp in rs1(c, d) + rs2(c, d):
                cp.wait_send()
        for d in range(side):
            ag3(c, d).wait_send()
        if c >= nc - 2:
            od(c).wait_send()


def solution(mesh):
    n = mesh.shape['dcp']
    side = math.isqrt(n // 2)

    def local(q, cache, lens):
        b, hl, k = q.shape
        t = cache.shape[1] * cache.shape[3]
        lorav = k - ROPE
        nb = min(8, max(1, b // 2))
        nc = b // nb
        tile = side * hl
        half = side * tile
        bf, f32 = jnp.bfloat16, jnp.float32
        dma = pltpu.SemaphoreType.DMA
        return pl.pallas_call(
            functools.partial(kernel, n, side, nc, nb, cache.shape[3]),
            out_shape=jax.ShapeDtypeStruct((b, hl, lorav), bf),
            in_specs=[pl.BlockSpec(memory_space=pltpu.VMEM), pl.BlockSpec(memory_space=pl.ANY),
                      pl.BlockSpec(memory_space=pltpu.SMEM)],
            out_specs=pl.BlockSpec(memory_space=pltpu.VMEM),
            scratch_shapes=[
                pltpu.VMEM((nc, side, nb, hl, k), bf),
                pltpu.VMEM((nc, 2 * side, nb, tile, k), bf),
                pltpu.VMEM((NBUF, t, k), bf),
                pltpu.VMEM((2, nb, half, lorav + LANES), f32),
                pltpu.VMEM((2, nb, half, lorav + LANES), f32),
                pltpu.VMEM((nc, nb, half, lorav + LANES), f32),
                pltpu.VMEM((nc, side, nb, tile, lorav), bf),
                pltpu.VMEM((nc, side, nb, tile, lorav), bf),
                pltpu.VMEM((nc, nb, LANES), f32),
                pltpu.VMEM((nc, side, nb, LANES), f32),
                pltpu.VMEM((nc, side, nb, hl, lorav), f32),
                pltpu.VMEM((nc, side, nb, hl, lorav), f32),
                pltpu.VMEM((nc, nb, LANES), f32),
                pltpu.VMEM((nc, side, nb, LANES), f32),
                pltpu.VMEM((side, nb, LANES), f32),
                dma((NBUF,)),
                dma((nc, side - 1)), dma((nc, side - 1)),
                dma((nc, side - 1)), dma((nc, side - 1)),
                dma((nc, side)), dma((nc, side)),
                dma((nc,)), dma((nc,)),
                dma((nc, side - 1)), dma((nc, side - 1)), dma((nc, side - 1)), dma((nc, side - 1)),
                dma((nc, side - 1)), dma((nc, side - 1)), dma((nc, side - 1)), dma((nc, side - 1)),
            ],
            compiler_params=pltpu.CompilerParams(collective_id=0, has_side_effects=True,
                                                 vmem_limit_bytes=63 * 1024 * 1024),
        )(q, cache.reshape(b, t, k), lens)

    return jax.shard_map(local, mesh=mesh, in_specs=(P('dp', 'dcp', None), P('dp', None, 'dcp', None, None), P('dp')),
                         out_specs=P('dp', 'dcp', None), check_vma=False)
```

time: 280 us -> 115 us (0.41)
  the two profiles are of different devices: /device:TPU:103 before, /device:TPU:96 now
where the time goes in v1:
time: 115 us; the launch traced here: 114 us
  Pallas kernels  112 us (97%)
  local copies, waits for them, and re-layouts  1.74 us (2%)
    pallas_call x1, Pallas kernels, local(): pl.pallas_call(functools.partial(kernel, n, side, nc, nb, cache.shape[3])...  112 us

profile of v1, /device:TPU:96, one launch (start us, length us, event | category | flops | bytes accessed | tf_op | source)
XLA Modules:
  0.0 113.7 jit_solution(503120547904932393)
XLA Ops:
  0.0 111.9 %shard_map.37 = bf16[64,4,512]{2,1,0:T(4,128)(2,1)} custom-call(bf16[64,4,576]{2,1,0:T(4,128)(2,1)} %q_ref.1, bf16[64,512,576]{2,1,0:T(8,128)(2,1)} %bitcast.1, s32[64]{0:T(128)} %lens_ref.1), custom_call_target="tpu_custom_call" | custom-call | tf_op jit(solution)/shard_map/pallas_call | solution.py:286
  111.9 1.7 %copy.5 = bf16[64,4,512]{2,1,0:T(4,128)(2,1)} copy(bf16[64,4,512]{2,1,0:T(4,128)(2,1)} %shard_map.37) | data formatting | bytes 524288

commit v2 on v1

--- a/solution.py
+++ b/solution.py
@@ -17,8 +17,8 @@
 
 
 def kernel(n, side, nc, nb, page, q_ref, cache_ref, lens_ref, out_ref,
-           g1, qall, cbuf, own, osend, orecv, p1s, p1r, l1s, l1r, p2s, p2r, l2s, l2r, wrow,
-           csem, a1s, a1r, a2s, a2r, a3s, a3r, ods, odr, s1, r1, sl1, rl1, s2, r2, sl2, rl2):
+           g1, qall, cbuf, own, osend, orecv, p1s, p1x, p1r, l1s, l1r, p2s, p2x, p2r, l2s, l2r, wrow,
+           csem, a1s, a1r, a2s, a2r, a3s, a3r, ods, odr, s1, r1, sl1, rr1, s2, r2, sl2, rr2):
     hl = q_ref.shape[1]
     k = q_ref.shape[2]
     t = cbuf.shape[1]
@@ -47,13 +47,30 @@
         return pltpu.make_async_remote_copy(src_ref=src, dst_ref=dst, send_sem=ss, recv_sem=rs, device_id=dev,
                                             device_id_type=pl.DeviceIdType.MESH)
 
-    def ag1(c, d):
-        (m1, peer), _ = axes(c)
-        return rcopy(q_ref.at[pl.ds(c * nb, nb)], g1.at[c, m1], a1s.at[c, d - 1], a1r.at[c, d - 1], peer(d))
-
-    def ag2(c, d):
-        _, (m2, peer) = axes(c)
-        return rcopy(qall.at[c, m2], qall.at[c, m2], a2s.at[c, d - 1], a2r.at[c, d - 1], peer(d))
+    hb = nb // 2
+
+    def part(h):
+        return pl.ds(h * hb, hb)
+
+    near = (1, side - 1)
+
+    def ag1(c, h):
+        (m1, peer), _ = axes(c)
+        return rcopy(q_ref.at[pl.ds(c * nb, nb)], g1.at[c, m1], a1s.at[c, h], a1r.at[c, h], peer(near[h]))
+
+    def ag1f(c, h):
+        (m1, peer), _ = axes(c)
+        a = (m1 + side - near[h]) % side
+        return rcopy(g1.at[c, a, part(h)], g1.at[c, a, part(h)], a1s.at[c, 2 + h], a1r.at[c, 2 + h], peer(near[h]))
+
+    def ag2(c, h):
+        _, (m2, peer) = axes(c)
+        return rcopy(qall.at[c, m2], qall.at[c, m2], a2s.at[c, h], a2r.at[c, h], peer(near[h]))
+
+    def ag2f(c, h):
+        _, (m2, peer) = axes(c)
+        a = (m2 + side - near[h]) % side
+        return rcopy(qall.at[c, a, part(h)], qall.at[c, a, part(h)], a2s.at[c, 2 + h], a2r.at[c, 2 + h], peer(near[h]))
 
     def ag3(c, d):
         _, (m2, _) = axes(c)
@@ -63,17 +80,39 @@
     def od(c):
         return rcopy(osend.at[c % 2], orecv.at[c], ods.at[c], odr.at[c], sib)
 
-    def rs1(c, d):
-        _, (m2, peer) = axes(c)
-        a = (m2 + d) % side
-        return (rcopy(p1s.at[c, a], p1r.at[c, m2], s1.at[c, d - 1], r1.at[c, d - 1], peer(d)),
-                rcopy(l1s.at[c], l1r.at[c, m2], sl1.at[c, d - 1], rl1.at[c, d - 1], peer(d)))
-
-    def rs2(c, d):
-        (m1, peer), _ = axes(c)
-        a = (m1 + d) % side
-        return (rcopy(p2s.at[c, a], p2r.at[c, m1], s2.at[c, d - 1], r2.at[c, d - 1], peer(d)),
-                rcopy(l2s.at[c], l2r.at[c, m1], sl2.at[c, d - 1], rl2.at[c, d - 1], peer(d)))
+    def rs1(c, h):
+        _, (m2, peer) = axes(c)
+        return rcopy(p1s.at[c, (m2 + near[h]) % side], p1r.at[c, m2], s1.at[c, h], r1.at[c, h], peer(near[h]))
+
+    def rs1x(c, h):
+        _, (m2, peer) = axes(c)
+        return rcopy(p1s.at[c, (m2 + 2) % side, part(h)], p1x.at[c, h], s1.at[c, 2 + h], r1.at[c, 2 + h], peer(near[h]))
+
+    def rs1f(c, h):
+        _, (m2, peer) = axes(c)
+        a = (m2 + side - near[h]) % side
+        return rcopy(p1x.at[c, h], p1r.at[c, a, part(h)], s1.at[c, 4 + h], r1.at[c, 4 + h], peer(near[h]))
+
+    def rl1(c, d):
+        _, (m2, peer) = axes(c)
+        return rcopy(l1s.at[c], l1r.at[c, m2], sl1.at[c, d - 1], rr1.at[c, d - 1], peer(d))
+
+    def rs2(c, h):
+        (m1, peer), _ = axes(c)
+        return rcopy(p2s.at[c, (m1 + near[h]) % side], p2r.at[c, m1], s2.at[c, h], r2.at[c, h], peer(near[h]))
+
+    def rs2x(c, h):
+        (m1, peer), _ = axes(c)
+        return rcopy(p2s.at[c, (m1 + 2) % side, part(h)], p2x.at[c, h], s2.at[c, 2 + h], r2.at[c, 2 + h], peer(near[h]))
+
+    def rs2f(c, h):
+        (m1, peer), _ = axes(c)
+        a = (m1 + side - near[h]) % side
+        return rcopy(p2x.at[c, h], p2r.at[c, a, part(h)], s2.at[c, 4 + h], r2.at[c, 4 + h], peer(near[h]))
+
+    def rl2(c, d):
+        (m1, peer), _ = axes(c)
+        return rcopy(l2s.at[c], l2r.at[c, m1], sl2.at[c, d - 1], rr2.at[c, d - 1], peer(d))
 
     def cload(b):
         return pltpu.make_async_copy(cache_ref.at[b], cbuf.at[b % NBUF], csem.at[b % NBUF])
@@ -87,16 +126,19 @@
         pl.semaphore_signal(barrier, inc=1, device_id=dev, device_id_type=pl.DeviceIdType.MESH)
     pl.semaphore_wait(barrier, len(peers))
 
-    order = sorted(dists, key=lambda d: min(d, side - d))
     for c in range(nc):
-        for d in order:
-            ag1(c, d).start()
+        for h in range(2):
+            ag1(c, h).start()
+    for c in range(nc):
+        for h in range(2):
+            ag1(c, h).wait_recv()
+            ag1f(c, h).start()
 
     def gather_first(c):
         (m1, _), (m2, _) = axes(c)
         g1[c, m1] = q_ref[pl.ds(c * nb, nb)]
-        for d in order:
-            ag1(c, d).wait_recv()
+        for h in range(2):
+            ag1f(c, h).wait_recv()
 
         def body(i, _):
             parts = [g1[c, a, i].astype(jnp.float32) for a in range(side)]
@@ -104,14 +146,20 @@
             return 0
 
         lax.fori_loop(0, nb, body, 0)
-        for d in order:
-            ag2(c, d).start()
+        for h in range(2):
+            ag2(c, h).start()
         ag3(c, 0).start()
 
     def gather_second(c):
-        for d in order:
-            ag2(c, d).wait_recv()
-            ag3(c, d).start()
+        for h in range(2):
+            ag2(c, h).wait_recv()
+            ag2f(c, h).start()
+            ag3(c, near[h]).start()
+
+    def gather_far(c):
+        for h in range(2):
+            ag2f(c, h).wait_recv()
+        ag3(c, 2).start()
 
     def gather_third(c):
         for d in range(side):
@@ -181,9 +229,17 @@
             return 0
 
         lax.fori_loop(0, nb, one, 0)
-        for d in order:
-            for cp in rs1(c, d):
-                cp.start()
+        for h in range(2):
+            rs1x(c, h).start()
+        for d in dists:
+            rl1(c, d).start()
+        for h in range(2):
+            rs1(c, h).start()
+
+    def pair_relay(c):
+        for h in range(2):
+            rs1x(c, h).wait_recv()
+            rs1f(c, h).start()
 
     def weights(ls):
         top = functools.reduce(jnp.maximum, ls)
@@ -209,9 +265,11 @@
 
     def second(c):
         (m1, _), (m2, _) = axes(c)
-        for d in order:
-            for cp in rs1(c, d):
-                cp.wait_recv()
+        for h in range(2):
+            rs1(c, h).wait_recv()
+            rs1f(c, h).wait_recv()
+        for d in dists:
+            rl1(c, d).wait_recv()
         idx = [(m2 + d) % side for d in dists]
         l2s[c] = weights([l1s[c]] + [l1r[c, a] for a in idx])
         srcs = [p1s.at[c, m2]] + [p1r.at[c, a] for a in idx]
@@ -223,15 +281,25 @@
             return 0
 
         lax.fori_loop(0, nb, one, 0)
-        for d in order:
-            for cp in rs2(c, d):
-                cp.start()
+        for h in range(2):
+            rs2x(c, h).start()
+        for d in dists:
+            rl2(c, d).start()
+        for h in range(2):
+            rs2(c, h).start()
+
+    def second_relay(c):
+        for h in range(2):
+            rs2x(c, h).wait_recv()
+            rs2f(c, h).start()
 
     def final(c):
         (m1, _), (m2, _) = axes(c)
-        for d in order:
-            for cp in rs2(c, d):
-                cp.wait_recv()
+        for h in range(2):
+            rs2(c, h).wait_recv()
+            rs2f(c, h).wait_recv()
+        for d in dists:
+            rl2(c, d).wait_recv()
         idx = [(m1 + d) % side for d in dists]
         weights([l2s[c]] + [l2r[c, a] for a in idx])
         srcs = [p2s.at[c, m1]] + [p2r.at[c, a] for a in idx]
@@ -242,27 +310,20 @@
 
         lax.fori_loop(0, nb, one, 0)
 
+    stages = ((gather_first, 6), (gather_second, 4), (gather_far, 1), (gather_third, 0), (compute, 0), (pair, -1),
+              (pair_relay, -2), (second, -3), (second_relay, -4), (final, -5))
+    for c in range(-6, nc + 5):
+        for stage, ahead in stages:
+            if 0 <= c + ahead < nc:
+                stage(c + ahead)
+
     for c in range(nc):
-        gather_first(c)
-    gather_second(0)
-    for c in range(nc + 3):
-        if c + 1 < nc:
-            gather_second(c + 1)
-        if c < nc:
-            gather_third(c)
-            compute(c)
-        if 0 <= c - 1 < nc:
-            pair(c - 1)
-        if 0 <= c - 2 < nc:
-            second(c - 2)
-        if 0 <= c - 3 < nc:
-            final(c - 3)
-    for c in range(nc):
-        for d in dists:
-            ag1(c, d).wait_send()
-            ag2(c, d).wait_send()
-            for cp in rs1(c, d) + rs2(c, d):
-                cp.wait_send()
+        for h in range(2):
+            for cp in (ag1, ag1f, ag2, ag2f, rs1, rs1x, rs1f, rs2, rs2x, rs2f):
+                cp(c, h).wait_send()
+        for d in dists:
+            rl1(c, d).wait_send()
+            rl2(c, d).wait_send()
         for d in range(side):
             ag3(c, d).wait_send()
         if c >= nc - 2:
@@ -297,21 +358,22 @@
                 pltpu.VMEM((2, nb, half, lorav + LANES), f32),
                 pltpu.VMEM((nc, nb, half, lorav + LANES), f32),
                 pltpu.VMEM((nc, side, nb, tile, lorav), bf),
+                pltpu.VMEM((nc, 2, nb // 2, tile, lorav), bf),
                 pltpu.VMEM((nc, side, nb, tile, lorav), bf),
                 pltpu.VMEM((nc, nb, LANES), f32),
                 pltpu.VMEM((nc, side, nb, LANES), f32),
                 pltpu.VMEM((nc, side, nb, hl, lorav), f32),
+                pltpu.VMEM((nc, 2, nb // 2, hl, lorav), f32),
                 pltpu.VMEM((nc, side, nb, hl, lorav), f32),
                 pltpu.VMEM((nc, nb, LANES), f32),
                 pltpu.VMEM((nc, side, nb, LANES), f32),
                 pltpu.VMEM((side, nb, LANES), f32),
                 dma((NBUF,)),
-                dma((nc, side - 1)), dma((nc, side - 1)),
-                dma((nc, side - 1)), dma((nc, side - 1)),
+                dma((nc, 4)), dma((nc, 4)), dma((nc, 4)), dma((nc, 4)),
                 dma((nc, side)), dma((nc, side)),
                 dma((nc,)), dma((nc,)),
-                dma((nc, side - 1)), dma((nc, side - 1)), dma((nc, side - 1)), dma((nc, side - 1)),
-                dma((nc, side - 1)), dma((nc, side - 1)), dma((nc, side - 1)), dma((nc, side - 1)),
+                dma((nc, 6)), dma((nc, 6)), dma((nc, side - 1)), dma((nc, side - 1)),
+                dma((nc, 6)), dma((nc, 6)), dma((nc, side - 1)), dma((nc, side - 1)),
             ],
             compiler_params=pltpu.CompilerParams(collective_id=0, has_side_effects=True,
                                                  vmem_limit_bytes=63 * 1024 * 1024),

time: 115 us -> 108 us (0.939)
  Pallas kernels: 112 us -> 105 us
    pallas_call x1, Pallas kernels: 112 us -> 105 us  [local(): pl.pallas_call(functools.partial(kernel, n, side, nc, nb, cache.shape[3])...]
where the time goes in v2:
time: 108 us; the launch traced here: 107 us
  Pallas kernels  105 us (97%)
  local copies, waits for them, and re-layouts  1.74 us (2%)
    pallas_call x1, Pallas kernels, local(): pl.pallas_call(functools.partial(kernel, n, side, nc, nb, cache.shape[3])...  105 us

profile of v2, /device:TPU:96, one launch (start us, length us, event | category | flops | bytes accessed | tf_op | source)
XLA Modules:
  0.0 106.9 jit_solution(4570862328417938845)
XLA Ops:
  0.0 105.1 %shard_map.37 = bf16[64,4,512]{2,1,0:T(4,128)(2,1)} custom-call(bf16[64,4,576]{2,1,0:T(4,128)(2,1)} %q_ref.1, bf16[64,512,576]{2,1,0:T(8,128)(2,1)} %bitcast.1, s32[64]{0:T(128)} %lens_ref.1), custom_call_target="tpu_custom_call" | custom-call | tf_op jit(solution)/shard_map/pallas_call | solution.py:347
  105.1 1.7 %copy.5 = bf16[64,4,512]{2,1,0:T(4,128)(2,1)} copy(bf16[64,4,512]{2,1,0:T(4,128)(2,1)} %shard_map.37) | data formatting | bytes 524288

commit v3 on v2

--- a/solution.py
+++ b/solution.py
@@ -14,6 +14,7 @@
 NEG = float('-inf')
 LANES = 128
 NBUF = 4
+NSLOT = 4
 
 
 def kernel(n, side, nc, nb, page, q_ref, cache_ref, lens_ref, out_ref,
@@ -39,9 +40,9 @@
     sib = at(y, x, 1 - core)
 
     def axes(c):
-        ax = (x, lambda d: at(y, (x + d) % side, core))
-        ay = (y, lambda d: at((y + d) % side, x, core))
-        return (ax, ay) if c % 2 == 0 else (ay, ax)
+        odd = c % 2
+        return ((x + odd * (y - x), lambda d: at((y + odd * d) % side, (x + (1 - odd) * d) % side, core)),
+                (y + odd * (x - y), lambda d: at((y + (1 - odd) * d) % side, (x + odd * d) % side, core)))
 
     def rcopy(src, dst, ss, rs, dev):
         return pltpu.make_async_remote_copy(src_ref=src, dst_ref=dst, send_sem=ss, recv_sem=rs, device_id=dev,
@@ -78,7 +79,7 @@
         return rcopy(qall.at[c, a], qall.at[c, side + a], a3s.at[c, d], a3r.at[c, d], sib)
 
     def od(c):
-        return rcopy(osend.at[c % 2], orecv.at[c], ods.at[c], odr.at[c], sib)
+        return rcopy(osend.at[c % NSLOT], orecv.at[c], ods.at[c], odr.at[c], sib)
 
     def rs1(c, h):
         _, (m2, peer) = axes(c)
@@ -126,10 +127,11 @@
         pl.semaphore_signal(barrier, inc=1, device_id=dev, device_id_type=pl.DeviceIdType.MESH)
     pl.semaphore_wait(barrier, len(peers))
 
-    for c in range(nc):
+    def gather_start(c):
         for h in range(2):
             ag1(c, h).start()
-    for c in range(nc):
+
+    def gather_relay(c):
         for h in range(2):
             ag1(c, h).wait_recv()
             ag1f(c, h).start()
@@ -169,8 +171,9 @@
     pos = (tpos // page) * (page * n) + me * page + tpos % page
 
     def compute(c):
-        if c >= 2:
-            od(c - 2).wait_send()
+        @pl.when(c >= NSLOT)
+        def _():
+            od(c - NSLOT).wait_send()
 
         def one(i, _):
             b = c * nb + i
@@ -189,10 +192,10 @@
             ls = jnp.where(l > 0.0, l, 1.0)
             o = acc * (1.0 / ls)
             lse = jnp.broadcast_to(jnp.where(l > 0.0, ms * SCALE + jnp.log(ls), NEG), (2 * half, LANES))
-            own[c % 2, i, :, :lorav] = o[:half]
-            own[c % 2, i, :, lorav:] = lse[:half]
-            osend[c % 2, i, :, :lorav] = o[half:]
-            osend[c % 2, i, :, lorav:] = lse[half:]
+            own[c % NSLOT, i, :, :lorav] = o[:half]
+            own[c % NSLOT, i, :, lorav:] = lse[:half]
+            osend[c % NSLOT, i, :, :lorav] = o[half:]
+            osend[c % NSLOT, i, :, lorav:] = lse[half:]
 
             @pl.when(b + NBUF < total)
             def _():
@@ -209,7 +212,7 @@
         od(c).wait_recv()
 
         def one(i, _):
-            la = own[c % 2, i, :, lorav:]
+            la = own[c % NSLOT, i, :, lorav:]
             lb = orecv[c, i, :, lorav:]
             top = jnp.maximum(la, lb)
             ts = jnp.where(top == NEG, 0.0, top)
@@ -222,7 +225,7 @@
             wb = wb * inv
             for j in range(lorav // LANES):
                 cols = slice(j * LANES, (j + 1) * LANES)
-                v = (wa * own[c % 2, i, :, cols] + wb * orecv[c, i, :, cols]).astype(jnp.bfloat16)
+                v = (wa * own[c % NSLOT, i, :, cols] + wb * orecv[c, i, :, cols]).astype(jnp.bfloat16)
                 p1s[c, :, i, :, cols] = v.reshape(side, tile, LANES)
             lse = jnp.where(ws > 0.0, ts + jnp.log(wss), NEG)
             l1s[c, pl.ds(i, 1)] = jnp.sum(jnp.where(diag, lse, 0.0), axis=0, keepdims=True)
@@ -310,14 +313,30 @@
 
         lax.fori_loop(0, nb, one, 0)
 
-    stages = ((gather_first, 6), (gather_second, 4), (gather_far, 1), (gather_third, 0), (compute, 0), (pair, -1),
-              (pair_relay, -2), (second, -3), (second_relay, -4), (final, -5))
-    for c in range(-6, nc + 5):
-        for stage, ahead in stages:
-            if 0 <= c + ahead < nc:
-                stage(c + ahead)
-
-    for c in range(nc):
+    def each(stage):
+        def one(c, _):
+            stage(c)
+            return 0
+
+        lax.fori_loop(0, nc, one, 0)
+
+    each(gather_start)
+    each(gather_relay)
+
+    stages = ((gather_first, 0), (gather_second, 6), (gather_far, 12), (gather_third, 14), (compute, 14), (pair, 16),
+              (pair_relay, 19), (second, 22), (second_relay, 26), (final, 30))
+
+    def step(i, _):
+        for stage, delay in stages:
+            @pl.when((i >= delay) & (i < delay + nc))
+            def _():
+                stage(jnp.maximum(i - delay, 0))
+
+        return 0
+
+    lax.fori_loop(0, nc + stages[-1][1], step, 0)
+
+    def drain(c):
         for h in range(2):
             for cp in (ag1, ag1f, ag2, ag2f, rs1, rs1x, rs1f, rs2, rs2x, rs2f):
                 cp(c, h).wait_send()
@@ -326,8 +345,12 @@
             rl2(c, d).wait_send()
         for d in range(side):
             ag3(c, d).wait_send()
-        if c >= nc - 2:
+
+        @pl.when(c >= nc - NSLOT)
+        def _():
             od(c).wait_send()
+
+    each(drain)
 
 
 def solution(mesh):
@@ -338,7 +361,7 @@
         b, hl, k = q.shape
         t = cache.shape[1] * cache.shape[3]
         lorav = k - ROPE
-        nb = min(8, max(1, b // 2))
+        nb = min(4, max(1, b // 2))
         nc = b // nb
         tile = side * hl
         half = side * tile
@@ -354,8 +377,8 @@
                 pltpu.VMEM((nc, side, nb, hl, k), bf),
                 pltpu.VMEM((nc, 2 * side, nb, tile, k), bf),
                 pltpu.VMEM((NBUF, t, k), bf),
-                pltpu.VMEM((2, nb, half, lorav + LANES), f32),
-                pltpu.VMEM((2, nb, half, lorav + LANES), f32),
+                pltpu.VMEM((NSLOT, nb, half, lorav + LANES), f32),
+                pltpu.VMEM((NSLOT, nb, half, lorav + LANES), f32),
                 pltpu.VMEM((nc, nb, half, lorav + LANES), f32),
                 pltpu.VMEM((nc, side, nb, tile, lorav), bf),
                 pltpu.VMEM((nc, 2, nb // 2, tile, lorav), bf),

time: 108 us -> 112 us (1.037)
  Pallas kernels: 105 us -> 110 us
    pallas_call x1, Pallas kernels: 105 us -> 110 us  [local(): pl.pallas_call(functools.partial(kernel, n, side, nc, nb, cache.shape[3])...]
where the time goes in v3:
time: 112 us
  Pallas kernels  110 us (98%)
  local copies, waits for them, and re-layouts  1.74 us (2%)
    pallas_call x1, Pallas kernels, local(): pl.pallas_call(functools.partial(kernel, n, side, nc, nb, cache.shape[3])...  110 us

profile of v3, /device:TPU:96, one launch (start us, length us, event | category | flops | bytes accessed | tf_op | source)
XLA Modules:
  0.0 111.9 jit_solution(4223849866419462040)
XLA Ops:
  0.0 110.2 %shard_map.37 = bf16[64,4,512]{2,1,0:T(4,128)(2,1)} custom-call(bf16[64,4,576]{2,1,0:T(4,128)(2,1)} %q_ref.1, bf16[64,512,576]{2,1,0:T(8,128)(2,1)} %bitcast.1, s32[64]{0:T(128)} %lens_ref.1), custom_call_target="tpu_custom_call" | custom-call | tf_op jit(solution)/shard_map/pallas_call | solution.py:370
  110.2 1.7 %copy.5 = bf16[64,4,512]{2,1,0:T(4,128)(2,1)} copy(bf16[64,4,512]{2,1,0:T(4,128)(2,1)} %shard_map.37) | data formatting | bytes 524288

commit v4 on v3

--- a/solution.py
+++ b/solution.py
@@ -13,12 +13,12 @@
 SCALE = QK_DIM ** -0.5
 NEG = float('-inf')
 LANES = 128
-NBUF = 4
+NBUF = 6
 NSLOT = 4
 
 
 def kernel(n, side, nc, nb, page, q_ref, cache_ref, lens_ref, out_ref,
-           g1, qall, cbuf, own, osend, orecv, p1s, p1x, p1r, l1s, l1r, p2s, p2x, p2r, l2s, l2r, wrow,
+           g1, qall, cbuf, own, osend, orecv, p1s, p1x, p1r, l1s, l1r, p2s, p2x, p2r, l2s, l2r, wrow, sb0, sb1,
            csem, a1s, a1r, a2s, a2r, a3s, a3r, ods, odr, s1, r1, sl1, rr1, s2, r2, sl2, rr2):
     hl = q_ref.shape[1]
     k = q_ref.shape[2]
@@ -170,40 +170,57 @@
     tpos = lax.broadcasted_iota(jnp.int32, (1, t), 1)
     pos = (tpos // page) * (page * n) + me * page + tpos % page
 
+    def scores(b, ref):
+        ref[...] = lax.dot_general(qall[b // nb, :, b % nb].reshape(2 * half, k), cbuf[b % NBUF],
+                                   (((1,), (1,)), ((), ())), preferred_element_type=jnp.float32)
+
+    def attend(c, i, ref):
+        b = c * nb + i
+        s = jnp.where(pos < lens_ref[b], ref[...], NEG)
+        m = jnp.max(s, axis=1, keepdims=True)
+        ms = jnp.where(m == NEG, 0.0, m)
+        p = jnp.exp((s - ms) * SCALE)
+        l = jnp.sum(p, axis=1, keepdims=True)
+        acc = lax.dot_general(p.astype(jnp.bfloat16), cbuf[b % NBUF, :, :lorav], (((1,), (0,)), ((), ())),
+                              preferred_element_type=jnp.float32)
+        ls = jnp.where(l > 0.0, l, 1.0)
+        o = acc * (1.0 / ls)
+        lse = jnp.broadcast_to(jnp.where(l > 0.0, ms * SCALE + jnp.log(ls), NEG), (2 * half, LANES))
+        own[c % NSLOT, i, :, :lorav] = o[:half]
+        own[c % NSLOT, i, :, lorav:] = lse[:half]
+        osend[c % NSLOT, i, :, :lorav] = o[half:]
+        osend[c % NSLOT, i, :, lorav:] = lse[half:]
+
     def compute(c):
         @pl.when(c >= NSLOT)
         def _():
             od(c - NSLOT).wait_send()
 
-        def one(i, _):
-            b = c * nb + i
-            slot = b % NBUF
-            cload(b).wait()
-            qb = qall[c, :, i].reshape(2 * half, k)
-            cb = cbuf[slot]
-            s = lax.dot_general(qb, cb, (((1,), (1,)), ((), ())), preferred_element_type=jnp.float32)
-            s = jnp.where(pos < lens_ref[b], s, NEG)
-            m = jnp.max(s, axis=1, keepdims=True)
-            ms = jnp.where(m == NEG, 0.0, m)
-            p = jnp.exp((s - ms) * SCALE)
-            l = jnp.sum(p, axis=1, keepdims=True)
-            acc = lax.dot_general(p.astype(jnp.bfloat16), cb[:, :lorav], (((1,), (0,)), ((), ())),
-                                  preferred_element_type=jnp.float32)
-            ls = jnp.where(l > 0.0, l, 1.0)
-            o = acc * (1.0 / ls)
-            lse = jnp.broadcast_to(jnp.where(l > 0.0, ms * SCALE + jnp.log(ls), NEG), (2 * half, LANES))
-            own[c % NSLOT, i, :, :lorav] = o[:half]
-            own[c % NSLOT, i, :, lorav:] = lse[:half]
-            osend[c % NSLOT, i, :, :lorav] = o[half:]
-            osend[c % NSLOT, i, :, lorav:] = lse[half:]
-
-            @pl.when(b + NBUF < total)
+        @pl.when(c == 0)
+        def _():
+            cload(0).wait()
+            scores(0, sb0)
+
+        def two(j, _):
+            b = c * nb + 2 * j
+            cload(b + 1).wait()
+
+            @pl.when(b + 2 < total)
             def _():
-                cload(b + NBUF).start()
-
-            return 0
-
-        lax.fori_loop(0, nb, one, 0)
+                cload(b + 2).wait()
+
+            scores(b + 1, sb1)
+            attend(c, 2 * j, sb0)
+            scores(jnp.minimum(b + 2, total - 1), sb0)
+            attend(c, 2 * j + 1, sb1)
+            for later in range(NBUF, NBUF + 2):
+                @pl.when(b + later < total)
+                def _():
+                    cload(b + later).start()
+
+            return 0
+
+        lax.fori_loop(0, nb // 2, two, 0)
         od(c).start()
 
     diag = lax.broadcasted_iota(jnp.int32, (half, LANES), 0) == lax.broadcasted_iota(jnp.int32, (half, LANES), 1)
@@ -323,7 +340,7 @@
     each(gather_start)
     each(gather_relay)
 
-    stages = ((gather_first, 0), (gather_second, 6), (gather_far, 12), (gather_third, 14), (compute, 14), (pair, 16),
+    stages = ((gather_first, 0), (gather_second, 6), (gather_far, 12), (gather_third, 13), (compute, 14), (pair, 16),
               (pair_relay, 19), (second, 22), (second_relay, 26), (final, 30))
 
     def step(i, _):
@@ -391,6 +408,7 @@
                 pltpu.VMEM((nc, nb, LANES), f32),
                 pltpu.VMEM((nc, side, nb, LANES), f32),
                 pltpu.VMEM((side, nb, LANES), f32),
+                pltpu.VMEM((2 * half, t), f32), pltpu.VMEM((2 * half, t), f32),
                 dma((NBUF,)),
                 dma((nc, 4)), dma((nc, 4)), dma((nc, 4)), dma((nc, 4)),
                 dma((nc, side)), dma((nc, side)),

time: 112 us -> 97.4 us (0.87)
  Pallas kernels: 110 us -> 95.4 us
    pallas_call x1, Pallas kernels: 110 us -> 95.4 us  [local(): pl.pallas_call(functools.partial(kernel, n, side, nc, nb, cache.shape[3])...]
where the time goes in v4:
time: 97.4 us; the launch traced here: 97.1 us
  Pallas kernels  95.4 us (98%)
  local copies, waits for them, and re-layouts  1.74 us (2%)
    pallas_call x1, Pallas kernels, local(): pl.pallas_call(functools.partial(kernel, n, side, nc, nb, cache.shape[3])...  95.4 us

profile of v4, /device:TPU:96, one launch (start us, length us, event | category | flops | bytes accessed | tf_op | source)
XLA Modules:
  0.0 97.1 jit_solution(16237397734700178947)
XLA Ops:
  0.0 95.4 %shard_map.37 = bf16[64,4,512]{2,1,0:T(4,128)(2,1)} custom-call(bf16[64,4,576]{2,1,0:T(4,128)(2,1)} %q_ref.1, bf16[64,512,576]{2,1,0:T(8,128)(2,1)} %bitcast.1, s32[64]{0:T(128)} %lens_ref.1), custom_call_target="tpu_custom_call" | custom-call | tf_op jit(solution)/shard_map/pallas_call | solution.py:387
  95.4 1.7 %copy.5 = bf16[64,4,512]{2,1,0:T(4,128)(2,1)} copy(bf16[64,4,512]{2,1,0:T(4,128)(2,1)} %shard_map.37) | data formatting | bytes 524288

commit v5 on v4

--- a/solution.py
+++ b/solution.py
@@ -27,6 +27,14 @@
     tile = side * hl
     half = side * tile
     total = nc * nb
+    each_type = total // 2
+
+    def row(c):
+        return (c // 2) * nb
+
+    def seq(b):
+        c = b // nb
+        return (c % 2) * each_type + row(c) + b % nb
 
     me = lax.axis_index('dcp')
     core = me % 2
@@ -55,14 +63,21 @@
 
     near = (1, side - 1)
 
-    def ag1(c, h):
-        (m1, peer), _ = axes(c)
-        return rcopy(q_ref.at[pl.ds(c * nb, nb)], g1.at[c, m1], a1s.at[c, h], a1r.at[c, h], peer(near[h]))
-
-    def ag1f(c, h):
-        (m1, peer), _ = axes(c)
+    bounds = [0, min(2 * nb, each_type), each_type]
+    pieces = [p for p in range(len(bounds) - 1) if bounds[p + 1] > bounds[p]]
+
+    def ag1(p, ty, h):
+        (m1, peer), _ = axes(ty)
+        at_ = pl.ds(bounds[p], bounds[p + 1] - bounds[p])
+        return rcopy(q_ref.at[pl.ds(ty * each_type + bounds[p], bounds[p + 1] - bounds[p])], g1.at[ty, m1, at_],
+                     a1s.at[p, ty, h], a1r.at[p, ty, h], peer(near[h]))
+
+    def ag1f(p, ty, h):
+        (m1, peer), _ = axes(ty)
         a = (m1 + side - near[h]) % side
-        return rcopy(g1.at[c, a, part(h)], g1.at[c, a, part(h)], a1s.at[c, 2 + h], a1r.at[c, 2 + h], peer(near[h]))
+        size = (bounds[p + 1] - bounds[p]) // 2
+        at_ = pl.ds(bounds[p] + h * size, size)
+        return rcopy(g1.at[ty, a, at_], g1.at[ty, a, at_], a1s.at[p, ty, 2 + h], a1r.at[p, ty, 2 + h], peer(near[h]))
 
     def ag2(c, h):
         _, (m2, peer) = axes(c)
@@ -94,9 +109,13 @@
         a = (m2 + side - near[h]) % side
         return rcopy(p1x.at[c, h], p1r.at[c, a, part(h)], s1.at[c, 4 + h], r1.at[c, 4 + h], peer(near[h]))
 
+    def both(c):
+        return pl.ds((c // 4) * 2, 2)
+
     def rl1(c, d):
         _, (m2, peer) = axes(c)
-        return rcopy(l1s.at[c], l1r.at[c, m2], sl1.at[c, d - 1], rr1.at[c, d - 1], peer(d))
+        return rcopy(l1s.at[c % 2, both(c)], l1r.at[c % 2, m2, both(c)], sl1.at[c % 2, c // 4, d - 1],
+                     rr1.at[c % 2, c // 4, d - 1], peer(d))
 
     def rs2(c, h):
         (m1, peer), _ = axes(c)
@@ -113,10 +132,11 @@
 
     def rl2(c, d):
         (m1, peer), _ = axes(c)
-        return rcopy(l2s.at[c], l2r.at[c, m1], sl2.at[c, d - 1], rr2.at[c, d - 1], peer(d))
+        return rcopy(l2s.at[c % 2, both(c)], l2r.at[c % 2, m1, both(c)], sl2.at[c % 2, c // 4, d - 1],
+                     rr2.at[c % 2, c // 4, d - 1], peer(d))
 
     def cload(b):
-        return pltpu.make_async_copy(cache_ref.at[b], cbuf.at[b % NBUF], csem.at[b % NBUF])
+        return pltpu.make_async_copy(cache_ref.at[seq(b)], cbuf.at[b % NBUF], csem.at[b % NBUF])
 
     for b in range(min(NBUF, total)):
         cload(b).start()
@@ -127,23 +147,33 @@
         pl.semaphore_signal(barrier, inc=1, device_id=dev, device_id_type=pl.DeviceIdType.MESH)
     pl.semaphore_wait(barrier, len(peers))
 
-    def gather_start(c):
-        for h in range(2):
-            ag1(c, h).start()
-
-    def gather_relay(c):
-        for h in range(2):
-            ag1(c, h).wait_recv()
-            ag1f(c, h).start()
+    def gather_far_rows(p):
+        for ty in range(2):
+            for h in range(2):
+                ag1f(p, ty, h).wait_recv()
+
+    for p in pieces:
+        for ty in range(2):
+            for h in range(2):
+                ag1(p, ty, h).start()
+    for p in pieces:
+        for ty in range(2):
+            (m1, _), _ = axes(ty)
+            g1[ty, m1, bounds[p]:bounds[p + 1]] = q_ref[ty * each_type + bounds[p]:ty * each_type + bounds[p + 1]]
+            for h in range(2):
+                ag1(p, ty, h).wait_recv()
+                ag1f(p, ty, h).start()
+    gather_far_rows(0)
 
     def gather_first(c):
-        (m1, _), (m2, _) = axes(c)
-        g1[c, m1] = q_ref[pl.ds(c * nb, nb)]
-        for h in range(2):
-            ag1f(c, h).wait_recv()
+        _, (m2, _) = axes(c)
+        if len(pieces) > 1:
+            @pl.when(c == 2 * bounds[1] // nb)
+            def _():
+                gather_far_rows(1)
 
         def body(i, _):
-            parts = [g1[c, a, i].astype(jnp.float32) for a in range(side)]
+            parts = [g1[c % 2, a, row(c) + i].astype(jnp.float32) for a in range(side)]
             qall[c, m2, i] = jnp.concatenate(parts, axis=0).astype(qall.dtype)
             return 0
 
@@ -176,7 +206,7 @@
 
     def attend(c, i, ref):
         b = c * nb + i
-        s = jnp.where(pos < lens_ref[b], ref[...], NEG)
+        s = jnp.where(pos < lens_ref[seq(b)], ref[...], NEG)
         m = jnp.max(s, axis=1, keepdims=True)
         ms = jnp.where(m == NEG, 0.0, m)
         p = jnp.exp((s - ms) * SCALE)
@@ -245,14 +275,18 @@
                 v = (wa * own[c % NSLOT, i, :, cols] + wb * orecv[c, i, :, cols]).astype(jnp.bfloat16)
                 p1s[c, :, i, :, cols] = v.reshape(side, tile, LANES)
             lse = jnp.where(ws > 0.0, ts + jnp.log(wss), NEG)
-            l1s[c, pl.ds(i, 1)] = jnp.sum(jnp.where(diag, lse, 0.0), axis=0, keepdims=True)
+            l1s[c % 2, c // 2, pl.ds(i, 1)] = jnp.sum(jnp.where(diag, lse, 0.0), axis=0, keepdims=True)
             return 0
 
         lax.fori_loop(0, nb, one, 0)
         for h in range(2):
             rs1x(c, h).start()
-        for d in dists:
-            rl1(c, d).start()
+
+        @pl.when((c // 2) % 2 == 1)
+        def _():
+            for d in dists:
+                rl1(c, d).start()
+
         for h in range(2):
             rs1(c, h).start()
 
@@ -288,10 +322,14 @@
         for h in range(2):
             rs1(c, h).wait_recv()
             rs1f(c, h).wait_recv()
-        for d in dists:
-            rl1(c, d).wait_recv()
+
+        @pl.when((c // 2) % 2 == 0)
+        def _():
+            for d in dists:
+                rl1(c, d).wait_recv()
+
         idx = [(m2 + d) % side for d in dists]
-        l2s[c] = weights([l1s[c]] + [l1r[c, a] for a in idx])
+        l2s[c % 2, c // 2] = weights([l1s[c % 2, c // 2]] + [l1r[c % 2, a, c // 2] for a in idx])
         srcs = [p1s.at[c, m2]] + [p1r.at[c, a] for a in idx]
 
         def one(i, _):
@@ -303,8 +341,12 @@
         lax.fori_loop(0, nb, one, 0)
         for h in range(2):
             rs2x(c, h).start()
-        for d in dists:
-            rl2(c, d).start()
+
+        @pl.when((c // 2) % 2 == 1)
+        def _():
+            for d in dists:
+                rl2(c, d).start()
+
         for h in range(2):
             rs2(c, h).start()
 
@@ -318,14 +360,18 @@
         for h in range(2):
             rs2(c, h).wait_recv()
             rs2f(c, h).wait_recv()
-        for d in dists:
-            rl2(c, d).wait_recv()
+
+        @pl.when((c // 2) % 2 == 0)
+        def _():
+            for d in dists:
+                rl2(c, d).wait_recv()
+
         idx = [(m1 + d) % side for d in dists]
-        weights([l2s[c]] + [l2r[c, a] for a in idx])
+        weights([l2s[c % 2, c // 2]] + [l2r[c % 2, a, c // 2] for a in idx])
         srcs = [p2s.at[c, m1]] + [p2r.at[c, a] for a in idx]
 
         def one(i, _):
-            out_ref[c * nb + i] = combine(i, hl, m2 * tile + m1 * hl, srcs).astype(out_ref.dtype)
+            out_ref[seq(c * nb + i)] = combine(i, hl, m2 * tile + m1 * hl, srcs).astype(out_ref.dtype)
             return 0
 
         lax.fori_loop(0, nb, one, 0)
@@ -337,11 +383,8 @@
 
         lax.fori_loop(0, nc, one, 0)
 
-    each(gather_start)
-    each(gather_relay)
-
-    stages = ((gather_first, 0), (gather_second, 6), (gather_far, 12), (gather_third, 13), (compute, 14), (pair, 16),
-              (pair_relay, 19), (second, 22), (second_relay, 26), (final, 30))
+    stages = ((gather_third, 10), (gather_first, 0), (compute, 11), (gather_second, 5), (pair_relay, 14),
+              (second_relay, 27), (gather_far, 8), (final, 38), (second, 18), (pair, 12))
 
     def step(i, _):
         for stage, delay in stages:
@@ -351,15 +394,19 @@
 
         return 0
 
-    lax.fori_loop(0, nc + stages[-1][1], step, 0)
+    lax.fori_loop(0, nc + max(d for _, d in stages), step, 0)
 
     def drain(c):
         for h in range(2):
-            for cp in (ag1, ag1f, ag2, ag2f, rs1, rs1x, rs1f, rs2, rs2x, rs2f):
+            for cp in (ag2, ag2f, rs1, rs1x, rs1f, rs2, rs2x, rs2f):
                 cp(c, h).wait_send()
-        for d in dists:
-            rl1(c, d).wait_send()
-            rl2(c, d).wait_send()
+
+        @pl.when((c // 2) % 2 == 1)
+        def _():
+            for d in dists:
+                rl1(c, d).wait_send()
+                rl2(c, d).wait_send()
+
         for d in range(side):
             ag3(c, d).wait_send()
 
@@ -368,6 +415,11 @@
             od(c).wait_send()
 
     each(drain)
+    for p in pieces:
+        for ty in range(2):
+            for h in range(2):
+                ag1(p, ty, h).wait_send()
+                ag1f(p, ty, h).wait_send()
 
 
 def solution(mesh):
@@ -378,7 +430,7 @@
         b, hl, k = q.shape
         t = cache.shape[1] * cache.shape[3]
         lorav = k - ROPE
-        nb = min(4, max(1, b // 2))
+        nb = min(4, max(1, b // 4))
         nc = b // nb
         tile = side * hl
         half = side * tile
@@ -391,7 +443,7 @@
                       pl.BlockSpec(memory_space=pltpu.SMEM)],
             out_specs=pl.BlockSpec(memory_space=pltpu.VMEM),
             scratch_shapes=[
-                pltpu.VMEM((nc, side, nb, hl, k), bf),
+                pltpu.VMEM((2, side, b // 2, hl, k), bf),
                 pltpu.VMEM((nc, 2 * side, nb, tile, k), bf),
                 pltpu.VMEM((NBUF, t, k), bf),
                 pltpu.VMEM((NSLOT, nb, half, lorav + LANES), f32),
@@ -400,21 +452,21 @@
                 pltpu.VMEM((nc, side, nb, tile, lorav), bf),
                 pltpu.VMEM((nc, 2, nb // 2, tile, lorav), bf),
                 pltpu.VMEM((nc, side, nb, tile, lorav), bf),
-                pltpu.VMEM((nc, nb, LANES), f32),
-                pltpu.VMEM((nc, side, nb, LANES), f32),
+                pltpu.VMEM((2, nc // 2, nb, LANES), f32),
+                pltpu.VMEM((2, side, nc // 2, nb, LANES), f32),
                 pltpu.VMEM((nc, side, nb, hl, lorav), f32),
                 pltpu.VMEM((nc, 2, nb // 2, hl, lorav), f32),
                 pltpu.VMEM((nc, side, nb, hl, lorav), f32),
-                pltpu.VMEM((nc, nb, LANES), f32),
-                pltpu.VMEM((nc, side, nb, LANES), f32),
+                pltpu.VMEM((2, nc // 2, nb, LANES), f32),
+                pltpu.VMEM((2, side, nc // 2, nb, LANES), f32),
                 pltpu.VMEM((side, nb, LANES), f32),
                 pltpu.VMEM((2 * half, t), f32), pltpu.VMEM((2 * half, t), f32),
                 dma((NBUF,)),
-                dma((nc, 4)), dma((nc, 4)), dma((nc, 4)), dma((nc, 4)),
+                dma((2, 2, 4)), dma((2, 2, 4)), dma((nc, 4)), dma((nc, 4)),
                 dma((nc, side)), dma((nc, side)),
                 dma((nc,)), dma((nc,)),
-                dma((nc, 6)), dma((nc, 6)), dma((nc, side - 1)), dma((nc, side - 1)),
-                dma((nc, 6)), dma((nc, 6)), dma((nc, side - 1)), dma((nc, side - 1)),
+                dma((nc, 6)), dma((nc, 6)), dma((2, nc // 4, side - 1)), dma((2, nc // 4, side - 1)),
+                dma((nc, 6)), dma((nc, 6)), dma((2, nc // 4, side - 1)), dma((2, nc // 4, side - 1)),
             ],
             compiler_params=pltpu.CompilerParams(collective_id=0, has_side_effects=True,
                                                  vmem_limit_bytes=63 * 1024 * 1024),

time: 97.4 us -> 94.5 us (0.970)
  Pallas kernels: 95.4 us -> 92.6 us
    pallas_call x1, Pallas kernels: 95.4 us -> 92.6 us  [local(): pl.pallas_call(functools.partial(kernel, n, side, nc, nb, cache.shape[3])...]
where the time goes in v5:
time: 94.5 us; the launch traced here: 94.3 us
  Pallas kernels  92.6 us (98%)
  local copies, waits for them, and re-layouts  1.74 us (2%)
    pallas_call x1, Pallas kernels, local(): pl.pallas_call(functools.partial(kernel, n, side, nc, nb, cache.shape[3])...  92.6 us

profile of v5, /device:TPU:96, one launch (start us, length us, event | category | flops | bytes accessed | tf_op | source)
XLA Modules:
  0.0 94.3 jit_solution(13034729162971898401)
XLA Ops:
  0.0 92.6 %shard_map.37 = bf16[64,4,512]{2,1,0:T(4,128)(2,1)} custom-call(bf16[64,4,576]{2,1,0:T(4,128)(2,1)} %q_ref.1, bf16[64,512,576]{2,1,0:T(8,128)(2,1)} %bitcast.1, s32[64]{0:T(128)} %lens_ref.1), custom_call_target="tpu_custom_call" | custom-call | tf_op jit(solution)/shard_map/pallas_call | solution.py:439
  92.6 1.7 %copy.5 = bf16[64,4,512]{2,1,0:T(4,128)(2,1)} copy(bf16[64,4,512]{2,1,0:T(4,128)(2,1)} %shard_map.37) | data formatting | bytes 524288

commit v6 on v5

--- a/solution.py
+++ b/solution.py
@@ -15,6 +15,7 @@
 LANES = 128
 NBUF = 6
 NSLOT = 4
+LAG = 2
 
 
 def kernel(n, side, nc, nb, page, q_ref, cache_ref, lens_ref, out_ref,
@@ -221,6 +222,27 @@
         osend[c % NSLOT, i, :, :lorav] = o[half:]
         osend[c % NSLOT, i, :, lorav:] = lse[half:]
 
+    diag = lax.broadcasted_iota(jnp.int32, (half, LANES), 0) == lax.broadcasted_iota(jnp.int32, (half, LANES), 1)
+
+    def pair_one(c, i):
+        la = own[c % NSLOT, i, :, lorav:]
+        lb = orecv[c, i, :, lorav:]
+        top = jnp.maximum(la, lb)
+        ts = jnp.where(top == NEG, 0.0, top)
+        wa = jnp.exp(la - ts)
+        wb = jnp.exp(lb - ts)
+        ws = wa + wb
+        wss = jnp.where(ws > 0.0, ws, 1.0)
+        inv = 1.0 / wss
+        wa = wa * inv
+        wb = wb * inv
+        for j in range(lorav // LANES):
+            cols = slice(j * LANES, (j + 1) * LANES)
+            v = (wa * own[c % NSLOT, i, :, cols] + wb * orecv[c, i, :, cols]).astype(jnp.bfloat16)
+            p1s[c, :, i, :, cols] = v.reshape(side, tile, LANES)
+        lse = jnp.where(ws > 0.0, ts + jnp.log(wss), NEG)
+        l1s[c % 2, c // 2, pl.ds(i, 1)] = jnp.sum(jnp.where(diag, lse, 0.0), axis=0, keepdims=True)
+
     def compute(c):
         @pl.when(c >= NSLOT)
         def _():
@@ -231,7 +253,7 @@
             cload(0).wait()
             scores(0, sb0)
 
-        def two(j, _):
+        def two(j, merged):
             b = c * nb + 2 * j
             cload(b + 1).wait()
 
@@ -240,6 +262,9 @@
                 cload(b + 2).wait()
 
             scores(b + 1, sb1)
+            if merged:
+                pair_one(jnp.maximum(c - LAG, 0), 2 * j)
+                pair_one(jnp.maximum(c - LAG, 0), 2 * j + 1)
             attend(c, 2 * j, sb0)
             scores(jnp.minimum(b + 2, total - 1), sb0)
             attend(c, 2 * j + 1, sb1)
@@ -250,35 +275,28 @@
 
             return 0
 
-        lax.fori_loop(0, nb // 2, two, 0)
+        @pl.when(c < LAG)
+        def _():
+            lax.fori_loop(0, nb // 2, lambda j, _: two(j, False), 0)
+
+        @pl.when(c >= LAG)
+        def _():
+            od(jnp.maximum(c - LAG, 0)).wait_recv()
+            lax.fori_loop(0, nb // 2, lambda j, _: two(j, True), 0)
+
         od(c).start()
 
-    diag = lax.broadcasted_iota(jnp.int32, (half, LANES), 0) == lax.broadcasted_iota(jnp.int32, (half, LANES), 1)
-
     def pair(c):
-        od(c).wait_recv()
-
-        def one(i, _):
-            la = own[c % NSLOT, i, :, lorav:]
-            lb = orecv[c, i, :, lorav:]
-            top = jnp.maximum(la, lb)
-            ts = jnp.where(top == NEG, 0.0, top)
-            wa = jnp.exp(la - ts)
-            wb = jnp.exp(lb - ts)
-            ws = wa + wb
-            wss = jnp.where(ws > 0.0, ws, 1.0)
-            inv = 1.0 / wss
-            wa = wa * inv
-            wb = wb * inv
-            for j in range(lorav // LANES):
-                cols = slice(j * LANES, (j + 1) * LANES)
-                v = (wa * own[c % NSLOT, i, :, cols] + wb * orecv[c, i, :, cols]).astype(jnp.bfloat16)
-                p1s[c, :, i, :, cols] = v.reshape(side, tile, LANES)
-            lse = jnp.where(ws > 0.0, ts + jnp.log(wss), NEG)
-            l1s[c % 2, c // 2, pl.ds(i, 1)] = jnp.sum(jnp.where(diag, lse, 0.0), axis=0, keepdims=True)
-            return 0
-
-        lax.fori_loop(0, nb, one, 0)
+        @pl.when(c >= nc - LAG)
+        def _():
+            od(c).wait_recv()
+
+            def one(i, _):
+                pair_one(c, i)
+                return 0
+
+            lax.fori_loop(0, nb, one, 0)
+
         for h in range(2):
             rs1x(c, h).start()
 
@@ -383,8 +401,8 @@
 
         lax.fori_loop(0, nc, one, 0)
 
-    stages = ((gather_third, 10), (gather_first, 0), (compute, 11), (gather_second, 5), (pair_relay, 14),
-              (second_relay, 27), (gather_far, 8), (final, 38), (second, 18), (pair, 12))
+    stages = ((gather_third, 12), (compute, 13), (pair, 15), (gather_first, 0), (pair_relay, 18), (gather_second, 5),
+              (gather_far, 9), (second, 23), (second_relay, 31), (final, 40))
 
     def step(i, _):
         for stage, delay in stages:

time: 94.5 us -> 93.7 us (level)
  no operation moved by 1% of the time
where the time goes in v6:
time: 93.7 us; the launch traced here: 93.6 us
  Pallas kernels  91.8 us (98%)
  local copies, waits for them, and re-layouts  1.74 us (2%)
    pallas_call x1, Pallas kernels, local(): pl.pallas_call(functools.partial(kernel, n, side, nc, nb, cache.shape[3])...  91.8 us

profile of v6, /device:TPU:96, one launch (start us, length us, event | category | flops | bytes accessed | tf_op | source)
XLA Modules:
  0.0 93.6 jit_solution(9745131064596447181)
XLA Ops:
  0.0 91.8 %shard_map.37 = bf16[64,4,512]{2,1,0:T(4,128)(2,1)} custom-call(bf16[64,4,576]{2,1,0:T(4,128)(2,1)} %q_ref.1, bf16[64,512,576]{2,1,0:T(8,128)(2,1)} %bitcast.1, s32[64]{0:T(128)} %lens_ref.1), custom_call_target="tpu_custom_call" | custom-call | tf_op jit(solution)/shard_map/pallas_call | solution.py:457
  91.8 1.7 %copy.5 = bf16[64,4,512]{2,1,0:T(4,128)(2,1)} copy(bf16[64,4,512]{2,1,0:T(4,128)(2,1)} %shard_map.37) | data formatting | bytes 524288

commit v7 on v6

--- a/solution.py
+++ b/solution.py
@@ -16,10 +16,11 @@
 NBUF = 6
 NSLOT = 4
 LAG = 2
+LAST = 4
 
 
 def kernel(n, side, nc, nb, page, q_ref, cache_ref, lens_ref, out_ref,
-           g1, qall, cbuf, own, osend, orecv, p1s, p1x, p1r, l1s, l1r, p2s, p2x, p2r, l2s, l2r, wrow, sb0, sb1,
+           g1, qall, cbuf, own, osend, orecv, p1s, p1x, p1r, l1s, l1r, p2s, p2x, p2r, l2s, l2r, wrow, sb0, sb1, ds, dr, dl, dlr, dsem,
            csem, a1s, a1r, a2s, a2r, a3s, a3r, ods, odr, s1, r1, sl1, rr1, s2, r2, sl2, rr2):
     hl = q_ref.shape[1]
     k = q_ref.shape[2]
@@ -143,7 +144,7 @@
         cload(b).start()
 
     barrier = pltpu.get_barrier_semaphore()
-    peers = [sib] + [at(y, (x + d) % side, core) for d in dists] + [at((y + d) % side, x, core) for d in dists]
+    peers = [sib] + [at((y + d // side) % side, (x + d % side) % side, core) for d in range(1, side * side)]
     for dev in peers:
         pl.semaphore_signal(barrier, inc=1, device_id=dev, device_id_type=pl.DeviceIdType.MESH)
     pl.semaphore_wait(barrier, len(peers))
@@ -224,7 +225,7 @@
 
     diag = lax.broadcasted_iota(jnp.int32, (half, LANES), 0) == lax.broadcasted_iota(jnp.int32, (half, LANES), 1)
 
-    def pair_one(c, i):
+    def pair_one(c, i, direct=False):
         la = own[c % NSLOT, i, :, lorav:]
         lb = orecv[c, i, :, lorav:]
         top = jnp.maximum(la, lb)
@@ -238,10 +239,18 @@
         wb = wb * inv
         for j in range(lorav // LANES):
             cols = slice(j * LANES, (j + 1) * LANES)
-            v = (wa * own[c % NSLOT, i, :, cols] + wb * orecv[c, i, :, cols]).astype(jnp.bfloat16)
-            p1s[c, :, i, :, cols] = v.reshape(side, tile, LANES)
+            v = wa * own[c % NSLOT, i, :, cols] + wb * orecv[c, i, :, cols]
+            if direct:
+                for a in range(side * side):
+                    ds[c - (nc - LAST), a, i, :, cols] = v[a * hl:(a + 1) * hl].astype(jnp.bfloat16)
+            else:
+                p1s[c, :, i, :, cols] = v.astype(jnp.bfloat16).reshape(side, tile, LANES)
         lse = jnp.where(ws > 0.0, ts + jnp.log(wss), NEG)
-        l1s[c % 2, c // 2, pl.ds(i, 1)] = jnp.sum(jnp.where(diag, lse, 0.0), axis=0, keepdims=True)
+        lrow = jnp.sum(jnp.where(diag, lse, 0.0), axis=0, keepdims=True)
+        if direct:
+            dl[c - (nc - LAST), pl.ds(i, 1)] = lrow
+        else:
+            l1s[c % 2, c // 2, pl.ds(i, 1)] = lrow
 
     def compute(c):
         @pl.when(c >= NSLOT)
@@ -275,28 +284,58 @@
 
             return 0
 
-        @pl.when(c < LAG)
+        merged = (c >= LAG) & (c < nc - LAST + LAG)
+
+        @pl.when(jnp.logical_not(merged))
         def _():
             lax.fori_loop(0, nb // 2, lambda j, _: two(j, False), 0)
 
-        @pl.when(c >= LAG)
+        @pl.when(merged)
         def _():
             od(jnp.maximum(c - LAG, 0)).wait_recv()
             lax.fori_loop(0, nb // 2, lambda j, _: two(j, True), 0)
 
         od(c).start()
 
+    def far_peer(c, k):
+        yy, xx = (y + k // side) % side, (x + k % side) % side
+        return c % 2 * (xx * side + yy) + (1 - c % 2) * (yy * side + xx), at(yy, xx, core)
+
+    def direct(c, k):
+        u = c - (nc - LAST)
+        slot, dev = far_peer(c, k)
+        return (rcopy(ds.at[u, slot], dr.at[u, k - 1], dsem.at[0, u], dsem.at[1, u], dev),
+                rcopy(dl.at[u], dlr.at[u, k - 1], dsem.at[2, u], dsem.at[3, u], dev))
+
+    def direct_all(u):
+        many = pl.ds(0, side * side - 1)
+        return (rcopy(ds.at[u, many], dr.at[u, many], dsem.at[0, u], dsem.at[1, u], sib),
+                rcopy(dlr.at[u, many], dlr.at[u, many], dsem.at[2, u], dsem.at[3, u], sib))
+
     def pair(c):
-        @pl.when(c >= nc - LAG)
-        def _():
-            od(c).wait_recv()
+        @pl.when(c < nc - LAST)
+        def _():
+            pair_send(c)
+
+        @pl.when(c >= nc - LAST)
+        def _():
+            tail = jnp.maximum(c, nc - LAST)
+            od(tail).wait_recv()
 
             def one(i, _):
-                pair_one(c, i)
+                pair_one(tail, i, direct=True)
                 return 0
 
             lax.fori_loop(0, nb, one, 0)
 
+            def send(k, _):
+                for cp in direct(tail, k):
+                    cp.start()
+                return 0
+
+            lax.fori_loop(1, side * side, send, 0)
+
+    def pair_send(c):
         for h in range(2):
             rs1x(c, h).start()
 
@@ -394,6 +433,21 @@
 
         lax.fori_loop(0, nb, one, 0)
 
+    def final_direct(c):
+        (m1, _), (m2, _) = axes(c)
+        u = c - (nc - LAST)
+        for cp in direct_all(u):
+            cp.wait_recv()
+        count = side * side - 1
+        weights([dl[u]] + [dlr[u, a] for a in range(count)])
+        srcs = [ds.at[u, m2 * side + m1]] + [dr.at[u, a] for a in range(count)]
+
+        def one(i, _):
+            out_ref[seq(c * nb + i)] = combine(i, hl, m2 * tile + m1 * hl, srcs).astype(out_ref.dtype)
+            return 0
+
+        lax.fori_loop(0, nb, one, 0)
+
     def each(stage):
         def one(c, _):
             stage(c)
@@ -401,38 +455,53 @@
 
         lax.fori_loop(0, nc, one, 0)
 
-    stages = ((gather_third, 12), (compute, 13), (pair, 15), (gather_first, 0), (pair_relay, 18), (gather_second, 5),
-              (gather_far, 9), (second, 23), (second_relay, 31), (final, 40))
+    mid = nc - LAST
+    stages = ((gather_third, 12, nc), (compute, 13, nc), (pair, 15, nc), (gather_first, 0, nc), (pair_relay, 18, mid),
+              (gather_second, 5, nc), (gather_far, 9, nc), (second, 23, mid), (second_relay, 29, mid), (final, 36, mid))
 
     def step(i, _):
-        for stage, delay in stages:
-            @pl.when((i >= delay) & (i < delay + nc))
+        for stage, delay, count in stages:
+            @pl.when((i >= delay) & (i < delay + count))
             def _():
                 stage(jnp.maximum(i - delay, 0))
 
         return 0
 
-    lax.fori_loop(0, nc + max(d for _, d in stages), step, 0)
+    lax.fori_loop(0, max(delay + count for _, delay, count in stages), step, 0)
+
+    def last(u, _):
+        final_direct(u + mid)
+        return 0
+
+    lax.fori_loop(0, LAST, last, 0)
 
     def drain(c):
         for h in range(2):
-            for cp in (ag2, ag2f, rs1, rs1x, rs1f, rs2, rs2x, rs2f):
-                cp(c, h).wait_send()
-
-        @pl.when((c // 2) % 2 == 1)
+            ag2(c, h).wait_send()
+            ag2f(c, h).wait_send()
+        for d in range(side):
+            ag3(c, d).wait_send()
+
+        @pl.when(c < mid)
+        def _():
+            for h in range(2):
+                for cp in (rs1, rs1x, rs1f, rs2, rs2x, rs2f):
+                    cp(c, h).wait_send()
+
+        @pl.when((c < mid) & ((c // 2) % 2 == 1))
         def _():
             for d in dists:
                 rl1(c, d).wait_send()
                 rl2(c, d).wait_send()
 
-        for d in range(side):
-            ag3(c, d).wait_send()
-
         @pl.when(c >= nc - NSLOT)
         def _():
             od(c).wait_send()
 
     each(drain)
+    for u in range(LAST):
+        for cp in direct_all(u):
+            cp.wait_send()
     for p in pieces:
         for ty in range(2):
             for h in range(2):
@@ -477,8 +546,13 @@
                 pltpu.VMEM((nc, side, nb, hl, lorav), f32),
                 pltpu.VMEM((2, nc // 2, nb, LANES), f32),
                 pltpu.VMEM((2, side, nc // 2, nb, LANES), f32),
-                pltpu.VMEM((side, nb, LANES), f32),
+                pltpu.VMEM((side * side, nb, LANES), f32),
                 pltpu.VMEM((2 * half, t), f32), pltpu.VMEM((2 * half, t), f32),
+                pltpu.VMEM((LAST, side * side, nb, hl, lorav), bf),
+                pltpu.VMEM((LAST, side * side - 1, nb, hl, lorav), bf),
+                pltpu.VMEM((LAST, nb, LANES), f32),
+                pltpu.VMEM((LAST, side * side - 1, nb, LANES), f32),
+                dma((4, LAST)),
                 dma((NBUF,)),
                 dma((2, 2, 4)), dma((2, 2, 4)), dma((nc, 4)), dma((nc, 4)),
                 dma((nc, side)), dma((nc, side)),

time: 93.7 us -> 101 us (1.078)
  Pallas kernels: 91.8 us -> 98.4 us
    pallas_call x1, Pallas kernels: 91.8 us -> 98.4 us  [local(): pl.pallas_call(functools.partial(kernel, n, side, nc, nb, cache.shape[3])...]
where the time goes in v7:
time: 101 us; the launch traced here: 100 us
  Pallas kernels  98.4 us (97%)
  local copies, waits for them, and re-layouts  1.74 us (2%)
    pallas_call x1, Pallas kernels, local(): pl.pallas_call(functools.partial(kernel, n, side, nc, nb, cache.shape[3])...  98.4 us

profile of v7, /device:TPU:96, one launch (start us, length us, event | category | flops | bytes accessed | tf_op | source)
XLA Modules:
  0.0 100.1 jit_solution(3553269562283683831)
XLA Ops:
  0.0 98.4 %shard_map.37 = bf16[64,4,512]{2,1,0:T(4,128)(2,1)} custom-call(bf16[64,4,576]{2,1,0:T(4,128)(2,1)} %q_ref.1, bf16[64,512,576]{2,1,0:T(8,128)(2,1)} %bitcast.1, s32[64]{0:T(128)} %lens_ref.1), custom_call_target="tpu_custom_call" | custom-call | tf_op jit(solution)/shard_map/pallas_call | solution.py:526
  98.4 1.7 %copy.5 = bf16[64,4,512]{2,1,0:T(4,128)(2,1)} copy(bf16[64,4,512]{2,1,0:T(4,128)(2,1)} %shard_map.37) | data formatting | bytes 524288

commit v8 on v6

--- a/solution.py
+++ b/solution.py
@@ -13,9 +13,17 @@
 SCALE = QK_DIM ** -0.5
 NEG = float('-inf')
 LANES = 128
-NBUF = 6
+NBUF = 8
 NSLOT = 4
 LAG = 2
+
+
+def mod(a, b):
+    return a % b if isinstance(a, int) else lax.rem(a, b)
+
+
+def div(a, b):
+    return a // b if isinstance(a, int) else lax.div(a, b)
 
 
 def kernel(n, side, nc, nb, page, q_ref, cache_ref, lens_ref, out_ref,
@@ -31,11 +39,11 @@
     each_type = total // 2
 
     def row(c):
-        return (c // 2) * nb
+        return (div(c, 2)) * nb
 
     def seq(b):
-        c = b // nb
-        return (c % 2) * each_type + row(c) + b % nb
+        c = div(b, nb)
+        return (mod(c, 2)) * each_type + row(c) + mod(b, nb)
 
     me = lax.axis_index('dcp')
     core = me % 2
@@ -48,10 +56,21 @@
 
     sib = at(y, x, 1 - core)
 
+    xs = [(x + d) % side for d in range(side)]
+    ys = [(y + d) % side for d in range(side)]
+    xid = [(y * side + v) * 2 + core for v in xs]
+    yid = [(v * side + x) * 2 + core for v in ys]
+
+    def pos_at(c, axis, d):
+        odd = mod(c, 2) if axis == 0 else 1 - mod(c, 2)
+        return xs[d] + odd * (ys[d] - xs[d])
+
     def axes(c):
-        odd = c % 2
-        return ((x + odd * (y - x), lambda d: at((y + odd * d) % side, (x + (1 - odd) * d) % side, core)),
-                (y + odd * (x - y), lambda d: at((y + (1 - odd) * d) % side, (x + odd * d) % side, core)))
+        def along(axis):
+            odd = mod(c, 2) if axis == 0 else 1 - mod(c, 2)
+            return pos_at(c, axis, 0), lambda d: {'dcp': xid[d] + odd * (yid[d] - xid[d])}
+
+        return along(0), along(1)
 
     def rcopy(src, dst, ss, rs, dev):
         return pltpu.make_async_remote_copy(src_ref=src, dst_ref=dst, send_sem=ss, recv_sem=rs, device_id=dev,
@@ -85,59 +104,58 @@
         return rcopy(qall.at[c, m2], qall.at[c, m2], a2s.at[c, h], a2r.at[c, h], peer(near[h]))
 
     def ag2f(c, h):
-        _, (m2, peer) = axes(c)
-        a = (m2 + side - near[h]) % side
+        _, (_, peer) = axes(c)
+        a = pos_at(c, 1, near[1 - h])
         return rcopy(qall.at[c, a, part(h)], qall.at[c, a, part(h)], a2s.at[c, 2 + h], a2r.at[c, 2 + h], peer(near[h]))
 
     def ag3(c, d):
-        _, (m2, _) = axes(c)
-        a = (m2 + side - d) % side
+        a = pos_at(c, 1, (side - d) % side)
         return rcopy(qall.at[c, a], qall.at[c, side + a], a3s.at[c, d], a3r.at[c, d], sib)
 
     def od(c):
-        return rcopy(osend.at[c % NSLOT], orecv.at[c], ods.at[c], odr.at[c], sib)
+        return rcopy(osend.at[mod(c, NSLOT)], orecv.at[c], ods.at[c], odr.at[c], sib)
 
     def rs1(c, h):
         _, (m2, peer) = axes(c)
-        return rcopy(p1s.at[c, (m2 + near[h]) % side], p1r.at[c, m2], s1.at[c, h], r1.at[c, h], peer(near[h]))
+        return rcopy(p1s.at[c, pos_at(c, 1, near[h])], p1r.at[c, m2], s1.at[c, h], r1.at[c, h], peer(near[h]))
 
     def rs1x(c, h):
         _, (m2, peer) = axes(c)
-        return rcopy(p1s.at[c, (m2 + 2) % side, part(h)], p1x.at[c, h], s1.at[c, 2 + h], r1.at[c, 2 + h], peer(near[h]))
+        return rcopy(p1s.at[c, pos_at(c, 1, 2), part(h)], p1x.at[c, h], s1.at[c, 2 + h], r1.at[c, 2 + h], peer(near[h]))
 
     def rs1f(c, h):
         _, (m2, peer) = axes(c)
-        a = (m2 + side - near[h]) % side
+        a = pos_at(c, 1, near[1 - h])
         return rcopy(p1x.at[c, h], p1r.at[c, a, part(h)], s1.at[c, 4 + h], r1.at[c, 4 + h], peer(near[h]))
 
     def both(c):
-        return pl.ds((c // 4) * 2, 2)
+        return pl.ds((div(c, 4)) * 2, 2)
 
     def rl1(c, d):
         _, (m2, peer) = axes(c)
-        return rcopy(l1s.at[c % 2, both(c)], l1r.at[c % 2, m2, both(c)], sl1.at[c % 2, c // 4, d - 1],
-                     rr1.at[c % 2, c // 4, d - 1], peer(d))
+        return rcopy(l1s.at[mod(c, 2), both(c)], l1r.at[mod(c, 2), m2, both(c)], sl1.at[mod(c, 2), div(c, 4), d - 1],
+                     rr1.at[mod(c, 2), div(c, 4), d - 1], peer(d))
 
     def rs2(c, h):
         (m1, peer), _ = axes(c)
-        return rcopy(p2s.at[c, (m1 + near[h]) % side], p2r.at[c, m1], s2.at[c, h], r2.at[c, h], peer(near[h]))
+        return rcopy(p2s.at[c, pos_at(c, 0, near[h])], p2r.at[c, m1], s2.at[c, h], r2.at[c, h], peer(near[h]))
 
     def rs2x(c, h):
         (m1, peer), _ = axes(c)
-        return rcopy(p2s.at[c, (m1 + 2) % side, part(h)], p2x.at[c, h], s2.at[c, 2 + h], r2.at[c, 2 + h], peer(near[h]))
+        return rcopy(p2s.at[c, pos_at(c, 0, 2), part(h)], p2x.at[c, h], s2.at[c, 2 + h], r2.at[c, 2 + h], peer(near[h]))
 
     def rs2f(c, h):
         (m1, peer), _ = axes(c)
-        a = (m1 + side - near[h]) % side
+        a = pos_at(c, 0, near[1 - h])
         return rcopy(p2x.at[c, h], p2r.at[c, a, part(h)], s2.at[c, 4 + h], r2.at[c, 4 + h], peer(near[h]))
 
     def rl2(c, d):
         (m1, peer), _ = axes(c)
-        return rcopy(l2s.at[c % 2, both(c)], l2r.at[c % 2, m1, both(c)], sl2.at[c % 2, c // 4, d - 1],
-                     rr2.at[c % 2, c // 4, d - 1], peer(d))
+        return rcopy(l2s.at[mod(c, 2), both(c)], l2r.at[mod(c, 2), m1, both(c)], sl2.at[mod(c, 2), div(c, 4), d - 1],
+                     rr2.at[mod(c, 2), div(c, 4), d - 1], peer(d))
 
     def cload(b):
-        return pltpu.make_async_copy(cache_ref.at[seq(b)], cbuf.at[b % NBUF], csem.at[b % NBUF])
+        return pltpu.make_async_copy(cache_ref.at[seq(b)], cbuf.at[mod(b, NBUF)], csem.at[mod(b, NBUF)])
 
     for b in range(min(NBUF, total)):
         cload(b).start()
@@ -174,7 +192,7 @@
                 gather_far_rows(1)
 
         def body(i, _):
-            parts = [g1[c % 2, a, row(c) + i].astype(jnp.float32) for a in range(side)]
+            parts = [g1[mod(c, 2), a, row(c) + i].astype(jnp.float32) for a in range(side)]
             qall[c, m2, i] = jnp.concatenate(parts, axis=0).astype(qall.dtype)
             return 0
 
@@ -202,7 +220,7 @@
     pos = (tpos // page) * (page * n) + me * page + tpos % page
 
     def scores(b, ref):
-        ref[...] = lax.dot_general(qall[b // nb, :, b % nb].reshape(2 * half, k), cbuf[b % NBUF],
+        ref[...] = lax.dot_general(qall[div(b, nb), :, mod(b, nb)].reshape(2 * half, k), cbuf[mod(b, NBUF)],
                                    (((1,), (1,)), ((), ())), preferred_element_type=jnp.float32)
 
     def attend(c, i, ref):
@@ -212,20 +230,20 @@
         ms = jnp.where(m == NEG, 0.0, m)
         p = jnp.exp((s - ms) * SCALE)
         l = jnp.sum(p, axis=1, keepdims=True)
-        acc = lax.dot_general(p.astype(jnp.bfloat16), cbuf[b % NBUF, :, :lorav], (((1,), (0,)), ((), ())),
+        acc = lax.dot_general(p.astype(jnp.bfloat16), cbuf[mod(b, NBUF), :, :lorav], (((1,), (0,)), ((), ())),
                               preferred_element_type=jnp.float32)
         ls = jnp.where(l > 0.0, l, 1.0)
         o = acc * (1.0 / ls)
         lse = jnp.broadcast_to(jnp.where(l > 0.0, ms * SCALE + jnp.log(ls), NEG), (2 * half, LANES))
-        own[c % NSLOT, i, :, :lorav] = o[:half]
-        own[c % NSLOT, i, :, lorav:] = lse[:half]
-        osend[c % NSLOT, i, :, :lorav] = o[half:]
-        osend[c % NSLOT, i, :, lorav:] = lse[half:]
+        own[mod(c, NSLOT), i, :, :lorav] = o[:half]
+        own[mod(c, NSLOT), i, :, lorav:] = lse[:half]
+        osend[mod(c, NSLOT), i, :, :lorav] = o[half:]
+        osend[mod(c, NSLOT), i, :, lorav:] = lse[half:]
 
     diag = lax.broadcasted_iota(jnp.int32, (half, LANES), 0) == lax.broadcasted_iota(jnp.int32, (half, LANES), 1)
 
     def pair_one(c, i):
-        la = own[c % NSLOT, i, :, lorav:]
+        la = own[mod(c, NSLOT), i, :, lorav:]
         lb = orecv[c, i, :, lorav:]
         top = jnp.maximum(la, lb)
         ts = jnp.where(top == NEG, 0.0, top)
@@ -238,15 +256,15 @@
         wb = wb * inv
         for j in range(lorav // LANES):
             cols = slice(j * LANES, (j + 1) * LANES)
-            v = (wa * own[c % NSLOT, i, :, cols] + wb * orecv[c, i, :, cols]).astype(jnp.bfloat16)
+            v = (wa * own[mod(c, NSLOT), i, :, cols] + wb * orecv[c, i, :, cols]).astype(jnp.bfloat16)
             p1s[c, :, i, :, cols] = v.reshape(side, tile, LANES)
         lse = jnp.where(ws > 0.0, ts + jnp.log(wss), NEG)
-        l1s[c % 2, c // 2, pl.ds(i, 1)] = jnp.sum(jnp.where(diag, lse, 0.0), axis=0, keepdims=True)
+        l1s[mod(c, 2), div(c, 2), pl.ds(i, 1)] = jnp.sum(jnp.where(diag, lse, 0.0), axis=0, keepdims=True)
 
     def compute(c):
         @pl.when(c >= NSLOT)
         def _():
-            od(c - NSLOT).wait_send()
+            od(jnp.maximum(c - NSLOT, 0)).wait_send()
 
         @pl.when(c == 0)
         def _():
@@ -300,7 +318,7 @@
         for h in range(2):
             rs1x(c, h).start()
 
-        @pl.when((c // 2) % 2 == 1)
+        @pl.when(mod(div(c, 2), 2) == 1)
         def _():
             for d in dists:
                 rl1(c, d).start()
@@ -341,13 +359,13 @@
             rs1(c, h).wait_recv()
             rs1f(c, h).wait_recv()
 
-        @pl.when((c // 2) % 2 == 0)
+        @pl.when(mod(div(c, 2), 2) == 0)
         def _():
             for d in dists:
                 rl1(c, d).wait_recv()
 
-        idx = [(m2 + d) % side for d in dists]
-        l2s[c % 2, c // 2] = weights([l1s[c % 2, c // 2]] + [l1r[c % 2, a, c // 2] for a in idx])
+        idx = [pos_at(c, 1, d) for d in dists]
+        l2s[mod(c, 2), div(c, 2)] = weights([l1s[mod(c, 2), div(c, 2)]] + [l1r[mod(c, 2), a, div(c, 2)] for a in idx])
         srcs = [p1s.at[c, m2]] + [p1r.at[c, a] for a in idx]
 
         def one(i, _):
@@ -360,7 +378,7 @@
         for h in range(2):
             rs2x(c, h).start()
 
-        @pl.when((c // 2) % 2 == 1)
+        @pl.when(mod(div(c, 2), 2) == 1)
         def _():
             for d in dists:
                 rl2(c, d).start()
@@ -379,13 +397,13 @@
             rs2(c, h).wait_recv()
             rs2f(c, h).wait_recv()
 
-        @pl.when((c // 2) % 2 == 0)
+        @pl.when(mod(div(c, 2), 2) == 0)
         def _():
             for d in dists:
                 rl2(c, d).wait_recv()
 
-        idx = [(m1 + d) % side for d in dists]
-        weights([l2s[c % 2, c // 2]] + [l2r[c % 2, a, c // 2] for a in idx])
+        idx = [pos_at(c, 0, d) for d in dists]
+        weights([l2s[mod(c, 2), div(c, 2)]] + [l2r[mod(c, 2), a, div(c, 2)] for a in idx])
         srcs = [p2s.at[c, m1]] + [p2r.at[c, a] for a in idx]
 
         def one(i, _):
@@ -419,7 +437,7 @@
             for cp in (ag2, ag2f, rs1, rs1x, rs1f, rs2, rs2x, rs2f):
                 cp(c, h).wait_send()
 
-        @pl.when((c // 2) % 2 == 1)
+        @pl.when(mod(div(c, 2), 2) == 1)
         def _():
             for d in dists:
                 rl1(c, d).wait_send()
@@ -449,7 +467,7 @@
         t = cache.shape[1] * cache.shape[3]
         lorav = k - ROPE
         nb = min(4, max(1, b // 4))
-        nc = b // nb
+        nc = div(b, nb)
         tile = side * hl
         half = side * tile
         bf, f32 = jnp.bfloat16, jnp.float32

time: 93.7 us -> 91.8 us (0.980)
  Pallas kernels: 91.8 us -> 90 us
    pallas_call x1, Pallas kernels: 91.8 us -> 90 us  [local(): pl.pallas_call(functools.partial(kernel, n, side, nc, nb, cache.shape[3])...]
where the time goes in v8:
time: 91.8 us; the launch traced here: 91.7 us
  Pallas kernels  90 us (98%)
  local copies, waits for them, and re-layouts  1.74 us (2%)
    pallas_call x1, Pallas kernels, local(): pl.pallas_call(functools.partial(kernel, n, side, nc, nb, cache.shape[3])...  90 us

profile of v8, /device:TPU:96, one launch (start us, length us, event | category | flops | bytes accessed | tf_op | source)
XLA Modules:
  0.0 91.7 jit_solution(17413307886144381582)
XLA Ops:
  0.0 90.0 %shard_map.37 = bf16[64,4,512]{2,1,0:T(4,128)(2,1)} custom-call(bf16[64,4,576]{2,1,0:T(4,128)(2,1)} %q_ref.1, bf16[64,512,576]{2,1,0:T(8,128)(2,1)} %bitcast.1, s32[64]{0:T(128)} %lens_ref.1), custom_call_target="tpu_custom_call" | custom-call | tf_op jit(solution)/shard_map/pallas_call | solution.py:475
  90.0 1.7 %copy.5 = bf16[64,4,512]{2,1,0:T(4,128)(2,1)} copy(bf16[64,4,512]{2,1,0:T(4,128)(2,1)} %shard_map.37) | data formatting | bytes 524288

commit v9 on v8

--- a/solution.py
+++ b/solution.py
@@ -26,8 +26,8 @@
     return a // b if isinstance(a, int) else lax.div(a, b)
 
 
-def kernel(n, side, nc, nb, page, q_ref, cache_ref, lens_ref, out_ref,
-           g1, qall, cbuf, own, osend, orecv, p1s, p1x, p1r, l1s, l1r, p2s, p2x, p2r, l2s, l2r, wrow, sb0, sb1,
+def kernel(n, side, nc, nb, page, q_hbm, cache_ref, lens_ref, out_ref,
+           q_ref, g1, qall, cbuf, own, osend, orecv, p1s, p1x, p1r, l1s, l1r, p2s, p2x, p2r, l2s, l2r, wrow, sb0, sb1,
            csem, a1s, a1r, a2s, a2r, a3s, a3r, ods, odr, s1, r1, sl1, rr1, s2, r2, sl2, rr2):
     hl = q_ref.shape[1]
     k = q_ref.shape[2]
@@ -157,6 +157,8 @@
     def cload(b):
         return pltpu.make_async_copy(cache_ref.at[seq(b)], cbuf.at[mod(b, NBUF)], csem.at[mod(b, NBUF)])
 
+    q_copy = pltpu.make_async_copy(q_hbm, q_ref, csem.at[NBUF])
+    q_copy.start()
     for b in range(min(NBUF, total)):
         cload(b).start()
 
@@ -165,6 +167,7 @@
     for dev in peers:
         pl.semaphore_signal(barrier, inc=1, device_id=dev, device_id_type=pl.DeviceIdType.MESH)
     pl.semaphore_wait(barrier, len(peers))
+    q_copy.wait()
 
     def gather_far_rows(p):
         for ty in range(2):
@@ -475,10 +478,11 @@
         return pl.pallas_call(
             functools.partial(kernel, n, side, nc, nb, cache.shape[3]),
             out_shape=jax.ShapeDtypeStruct((b, hl, lorav), bf),
-            in_specs=[pl.BlockSpec(memory_space=pltpu.VMEM), pl.BlockSpec(memory_space=pl.ANY),
+            in_specs=[pl.BlockSpec(memory_space=pl.ANY), pl.BlockSpec(memory_space=pl.ANY),
                       pl.BlockSpec(memory_space=pltpu.SMEM)],
             out_specs=pl.BlockSpec(memory_space=pltpu.VMEM),
             scratch_shapes=[
+                pltpu.VMEM((b, hl, k), bf),
                 pltpu.VMEM((2, side, b // 2, hl, k), bf),
                 pltpu.VMEM((nc, 2 * side, nb, tile, k), bf),
                 pltpu.VMEM((NBUF, t, k), bf),
@@ -497,7 +501,7 @@
                 pltpu.VMEM((2, side, nc // 2, nb, LANES), f32),
                 pltpu.VMEM((side, nb, LANES), f32),
                 pltpu.VMEM((2 * half, t), f32), pltpu.VMEM((2 * half, t), f32),
-                dma((NBUF,)),
+                dma((NBUF + 1,)),
                 dma((2, 2, 4)), dma((2, 2, 4)), dma((nc, 4)), dma((nc, 4)),
                 dma((nc, side)), dma((nc, side)),
                 dma((nc,)), dma((nc,)),

time: 91.8 us -> 91.5 us (level)
  no operation moved by 1% of the time
where the time goes in v9:
time: 91.5 us; the launch traced here: 91.4 us
  Pallas kernels  89.7 us (98%)
  local copies, waits for them, and re-layouts  1.74 us (2%)
    pallas_call x1, Pallas kernels, local(): pl.pallas_call(functools.partial(kernel, n, side, nc, nb, cache.shape[3])...  89.7 us

profile of v9, /device:TPU:96, one launch (start us, length us, event | category | flops | bytes accessed | tf_op | source)
XLA Modules:
  0.0 91.4 jit_solution(15348984531340384447)
XLA Ops:
  0.0 89.7 %shard_map.37 = bf16[64,4,512]{2,1,0:T(4,128)(2,1)} custom-call(bf16[64,4,576]{2,1,0:T(4,128)(2,1)} %q_hbm.1, bf16[64,512,576]{2,1,0:T(8,128)(2,1)} %bitcast.1, s32[64]{0:T(128)} %lens_ref.1), custom_call_target="tpu_custom_call" | custom-call | tf_op jit(solution)/shard_map/pallas_call | solution.py:478
  89.7 1.7 %copy.5 = bf16[64,4,512]{2,1,0:T(4,128)(2,1)} copy(bf16[64,4,512]{2,1,0:T(4,128)(2,1)} %shard_map.37) | data formatting | bytes 524288
